TPU v7x, 32 devices: a whole 2x2x4 slice. The times are simulated.
32 devices in a mesh: lat: 8 (over z, x), lon: 4 (over y, core).
Axes of the slice: x: 2, y: 2, z: 4, core: 2. Of those that a mesh axis runs over, the one named last changes fastest.
Arguments:
- courant: float32 [2, 16, 128, 512], P(None, None, 'lat', 'lon'), may hold values from -0.45 to 0.45
- obs_matrix: float32 [8, 32, 128, 128], P('lat', 'lon'), may hold values from -0.5 to 0.5
- obs_weight: float32 [8, 32, 128], P('lat', 'lon'), may hold values from 0.5 to 4
- innovation: float32 [8, 32, 128], P('lat', 'lon'), may hold values from -6 to 6
- block_owner: int32 [8, 32, 1], P('lat', 'lon'), may hold values from 0 to 3; in each aligned block of 8 rows (0 to 7, 8 to 15, ..., all dimensions but the last counted through in order) at most 2 rows name the same one
- block_row: int32 [8, 32], P('lat', 'lon'), may hold values from 0 to 255
- block_count: int32 [8, 4], P('lat', 'lon'), may hold values from 1 to 8, as said below
Outputs:
- increment: float32 [16, 128, 512], P(None, 'lat', 'lon')
- residual: float32 [16, 128, 512], P(None, 'lat', 'lon')
Inputs may be any that keep to these rules, and one draw needn't show every extreme that they name: `block_owner`: among one device's 8 block slots no lon index is named more than 2 times, a bound that some block reaches. A device's first block_count slots are live, the rest are padding; some device has all 8 live.
All inputs are finite; a program needn't handle non-finite values.
Results may differ from a plain program's by a relative error of at most 0.0003.
Values sent between devices are 32-bit elements; how exact they have to be, the bound alone decides.
A program may use at most 64 MiB of HBM per device.

v0:
```python
import functools

import jax
import jax.numpy as jnp
from jax import lax
from jax.experimental import pallas as pl
from jax.experimental.pallas import tpu as pltpu
from jax.sharding import PartitionSpec as P

STEPS = 4
HALO = 2 * STEPS
MESH = pl.DeviceIdType.MESH
F32 = jnp.float32
BF16 = jnp.bfloat16


def split3(x):
    hi = x.astype(BF16)
    rest = x - hi.astype(F32)
    mid = rest.astype(BF16)
    low = (rest - mid.astype(F32)).astype(BF16)
    return hi, mid, low


def dot3(onehot, x):
    total = None
    for part in split3(x):
        term = jnp.dot(onehot, part, preferred_element_type=F32)
        total = term if total is None else total + term
    return total


def kernel(
    n_lat, n_lon,
    courant, obs, weight_in, innov_in, owner_in, row_in, count_in,
    parts_o, alpha1_out, left1_out, alpha2_out, beta_out,
    flow, rate_in,
    rates, obs_v, terms, codes, code_out, spread_mat, gather_mat,
    field, moved, parts_t, fetch_out, fetch_in, red_lon, red_lat,
    obs_sem, own_sem, flow_sem, wide_send, wide_recv, fetch_send, fetch_recv, part_send, part_recv,
    lon_send, lon_recv, lat_send, lat_recv,
    weight, innov, owner, row, count, input_sems,
):
    li = lax.axis_index("lat")
    lo = lax.axis_index("lon")
    _, levels, clat, clon = parts_o.shape
    cap = obs_v.shape[0]
    share = levels // n_lon
    ext = clat + 2 * HALO
    tile_rows = n_lon * ext
    n_src = 3 * n_lon

    flow_copy = pltpu.make_async_copy(courant, flow, flow_sem)
    flow_copy.start()
    small = [
        pltpu.make_async_copy(src, dst, input_sems.at[n])
        for n, (src, dst) in enumerate((
            (owner_in, owner), (row_in, row), (count_in, count), (weight_in, weight), (innov_in, innov)))
    ]
    for copy in small:
        copy.start()
    obs_copy = pltpu.make_async_copy(obs.at[0], obs_v, obs_sem)
    obs_copy.start()

    def exists(d):
        return (li + d >= 0) & (li + d < n_lat)

    def guarded(d, run):
        if d == 0:
            run()
        else:
            pl.when(exists(d))(run)

    def lon_at(j):
        return lax.rem(lo + j + n_lon, n_lon)

    barrier = pltpu.get_barrier_semaphore()

    def greet(lat, lon):
        pl.semaphore_signal(barrier, inc=1, device_id={"lat": lat, "lon": lon}, device_id_type=MESH)

    @pl.loop(1, n_lat)
    def _(j):
        greet(lax.rem(li + j, n_lat), lo)

    for d in (-1, 1):
        def hello(d=d):
            for j in range(1, n_lon):
                greet(li + d, lon_at(j))
        guarded(d, hello)
    for j in range(1, n_lon):
        greet(li, lon_at(j))

    for copy in small:
        copy.wait()

    sub = lax.broadcasted_iota(jnp.int32, (cap, clon), 0)
    live = count[0, 0]
    scal = []
    for b in range(cap):
        r = row[0, b]
        lev = lax.div(r, jnp.int32(clat))
        scal.append((r - lev * clat, (lev * n_lon + owner[0, b]) * ext))
    for d in (-1, 0, 1):
        tile = jnp.full((cap, clon), -1, jnp.int32)
        for b in range(cap):
            lat_local = scal[b][0] + (HALO - clat * d)
            ok = (lat_local >= 0) & (lat_local < ext) & (b < live)
            tile = jnp.where(sub == b, jnp.where(ok, scal[b][1] + lat_local, -1), tile)
        code_out[d + 1] = tile.astype(F32)

    sides = (li > 0).astype(jnp.int32) + (li < n_lat - 1).astype(jnp.int32)
    pl.semaphore_wait(barrier, (n_lon - 1) + (n_lat - 1) + sides * (n_lon - 1))

    def wide(kind, d, j, src, dst):
        return pltpu.make_async_remote_copy(
            src_ref=src, dst_ref=dst,
            send_sem=wide_send.at[kind, d + 1, j], recv_sem=wide_recv.at[kind, d + 1, j],
            device_id={"lat": li + d, "lon": lon_at(j)}, device_id_type=MESH,
        )

    def send_slot(d):
        return (1 - d) * n_lon + lo

    def recv_slot(d, j):
        return (1 - d) * n_lon + lon_at(-j)

    def code_copy(d, j, slot):
        return wide(0, d, j, code_out.at[d + 1], codes.at[slot])

    def rate_copy(d, j, peer, tile):
        levs = pl.ds(peer * share, share)
        if d == 0:
            src, dst = pl.ds(0, clat), pl.ds(HALO, clat)
        elif d == 1:
            src, dst = pl.ds(clat - HALO, HALO), pl.ds(0, HALO)
        else:
            src, dst = pl.ds(0, HALO), pl.ds(HALO + clat, HALO)
        return wide(1, d, j, flow.at[:, levs, src, :], rate_in.at[:, :, tile, dst, :])

    def term_copy(rnd, d, j, slot):
        return wide(2 + rnd, d, j, terms.at[rnd, n_lon + lo], terms.at[rnd, slot])

    def start_wide(make):
        for d in (-1, 1, 0):
            def run(d=d):
                for j in range(n_lon):
                    if (d, j) != (0, 0):
                        make(d, j, True).start()
            guarded(d, run)

    def recv_wide(make):
        for d in (-1, 1, 0):
            def run(d=d):
                for j in range(n_lon):
                    if (d, j) != (0, 0):
                        make(d, j, False).wait_recv()
            guarded(-d, run)

    def done_wide(make):
        for d in (-1, 1, 0):
            def run(d=d):
                for j in range(n_lon):
                    if (d, j) != (0, 0):
                        make(d, j, True).wait_send()
            guarded(d, run)

    def code_make(d, j, out):
        return code_copy(d, j, send_slot(d) if out else recv_slot(d, j))

    def rate_make(d, j, out):
        return rate_copy(d, j, lon_at(j), lo if out else lon_at(-j))

    def term_make(rnd):
        return lambda d, j, out: term_copy(rnd, d, j, send_slot(d) if out else recv_slot(d, j))

    own_rate = pltpu.make_async_copy(
        flow.at[:, pl.ds(lo * share, share), :, :],
        rate_in.at[:, :, lo, pl.ds(HALO, clat), :], own_sem)
    flow_copy.wait()
    start_wide(rate_make)
    start_wide(code_make)
    own_rate.start()
    codes[n_lon + lo] = code_out[1]

    pad = codes.shape[0] - n_src
    none = jnp.full((n_lon, cap, clon), -1.0, F32)
    if pad:
        codes[n_src:] = jnp.full((pad, cap, clon), -1.0, F32)
        for rnd in range(3):
            terms[rnd, n_src:] = jnp.zeros((pad, cap, clon), F32)
    for d in (-1, 1):
        @pl.when(jnp.logical_not(exists(d)))
        def _(d=d):
            first = (d + 1) * n_lon
            codes[first:first + n_lon] = none
            for rnd in range(3):
                terms[rnd, first:first + n_lon] = jnp.zeros((n_lon, cap, clon), F32)
            lat0 = 0 if d == -1 else HALO + clat
            rate_in[:, :, :, lat0:lat0 + HALO, :] = jnp.zeros((2, share, n_lon, HALO, clon), F32)

    live_rows = sub < live
    w_rows = jnp.where(live_rows, weight[0], 0.0)
    wy_rows = w_rows * innov[0]
    stacked = jnp.concatenate([w_rows, wy_rows, jnp.zeros((clon - 2 * cap, clon), F32)], axis=0)
    columns = jnp.transpose(stacked)
    w_col = [columns[:, b:b + 1] for b in range(cap)]

    def spread(rnd, u_cols):
        out = [jnp.sum(obs_v[b] * u_cols[b], axis=0, keepdims=True) for b in range(cap)]
        terms[rnd, n_lon + lo] = jnp.concatenate(out, axis=0)
        start_wide(term_make(rnd))

    obs_copy.wait()
    spread(0, [columns[:, cap + b:cap + b + 1] for b in range(cap)])

    base = (lo * (share * tile_rows)).astype(F32)
    recv_wide(code_make)
    n_blocks = codes.shape[0] * cap
    flat_codes = codes[...].reshape(n_blocks, clon) - base
    code_row = jnp.transpose(flat_codes)[0:1, :]
    for k in range(share):
        place = lax.broadcasted_iota(jnp.int32, (tile_rows, n_blocks), 0).astype(F32) + float(k * tile_rows)
        spread_mat[k * tile_rows:(k + 1) * tile_rows, :] = jnp.where(place == code_row, 1.0, 0.0).astype(BF16)
    centre = flat_codes[n_lon * cap:2 * n_lon * cap, :]
    for c in range(share * tile_rows // clon):
        lane_place = lax.broadcasted_iota(jnp.int32, centre.shape, 1).astype(F32) + float(c * clon)
        gather_mat[:, c * clon:(c + 1) * clon] = jnp.where(lane_place == centre, 1.0, 0.0).astype(BF16)

    recv_wide(rate_make)
    own_rate.wait()
    for k in range(share):
        c0 = rate_in[0, k].reshape(tile_rows, clon)
        c1 = rate_in[1, k].reshape(tile_rows, clon)
        a, b = jnp.maximum(c0, 0.0), jnp.maximum(-c0, 0.0)
        e, f = jnp.maximum(c1, 0.0), jnp.maximum(-c1, 0.0)
        rates[0, k], rates[1, k], rates[2, k], rates[3, k] = a, b, e, f
        rates[4, k] = 1.0 - a - b - e - f

    lane = lax.broadcasted_iota(jnp.int32, (tile_rows, clon), 1)
    lat_ids = lax.broadcasted_iota(jnp.int32, (ext, clon), 0) + (li * clat - HALO)
    inside = jnp.where((lat_ids >= 0) & (lat_ids < n_lat * clat), 1.0, 0.0)
    inside = jnp.concatenate([inside] * n_lon, axis=0)

    def lat_up(x):
        return pltpu.roll(x, tile_rows - 1, 0)

    def lat_down(x):
        return pltpu.roll(x, 1, 0)

    def lon_up(x):
        xs = pltpu.roll(x, clon - 1, 1)
        return jnp.where(lane == clon - 1, jnp.concatenate([xs[ext:], xs[:ext]], axis=0), xs)

    def lon_down(x):
        xs = pltpu.roll(x, 1, 1)
        return jnp.where(lane == 0, jnp.concatenate([xs[-ext:], xs[:-ext]], axis=0), xs)

    def apply_model(rnd, forward):
        flat = dot3(spread_mat[...], terms[rnd].reshape(n_blocks, clon))
        field[...] = flat.reshape(share, tile_rows, clon)

        @pl.loop(0, share, unroll=share)
        def _(k):
            y = field[k]
            for _ in range(STEPS):
                y = (rates[4, k] * y + lat_up(rates[0, k] * y) + lat_down(rates[1, k] * y)
                     + lon_up(rates[2, k] * y) + lon_down(rates[3, k] * y))
            for t in range(n_lon):
                parts_t[rnd, t, k] = y[t * ext + HALO:t * ext + HALO + clat]
            if forward:
                x = y * inside
                for _ in range(STEPS):
                    x = (rates[4, k] * x + rates[0, k] * lat_down(x) + rates[1, k] * lat_up(x)
                         + rates[2, k] * lon_down(x) + rates[3, k] * lon_up(x))
                moved[k] = x

    def part_make(rnd, j, out):
        place = lo if out else lon_at(-j)
        return pltpu.make_async_remote_copy(
            src_ref=parts_t.at[rnd, lon_at(j)],
            dst_ref=parts_o.at[rnd, pl.ds(place * share, share)],
            send_sem=part_send.at[rnd, j], recv_sem=part_recv.at[rnd, j],
            device_id={"lat": li, "lon": lon_at(j)}, device_id_type=MESH)

    def send_parts(rnd):
        for j in range(1, n_lon):
            part_make(rnd, j, True).start()
        parts_o[rnd, pl.ds(lo * share, share)] = parts_t[rnd, lo]

    def fetch_make(rnd, j, out):
        place = lo if out else lon_at(-j)
        return pltpu.make_async_remote_copy(
            src_ref=fetch_out.at[rnd, lon_at(j)], dst_ref=fetch_in.at[rnd, place],
            send_sem=fetch_send.at[rnd, j], recv_sem=fetch_recv.at[rnd, j],
            device_id={"lat": li, "lon": lon_at(j)}, device_id_type=MESH)

    def send_fetch(rnd):
        seen = dot3(gather_mat[...], moved[...].reshape(share * tile_rows, clon))
        fetch_out[rnd] = seen.reshape(n_lon, cap, clon)
        for j in range(1, n_lon):
            fetch_make(rnd, j, True).start()
        fetch_in[rnd, lo] = fetch_out[rnd, lo]

    def observe(rnd):
        for j in range(1, n_lon):
            fetch_make(rnd, j, False).wait_recv()
        seen = jnp.sum(fetch_in[rnd], axis=0)
        return [jnp.sum(obs_v[b] * seen[b:b + 1, :], axis=1, keepdims=True) for b in range(cap)]

    def red_lon_make(rnd, j, out):
        return pltpu.make_async_remote_copy(
            src_ref=red_lon.at[rnd, lo], dst_ref=red_lon.at[rnd, lo if out else lon_at(-j)],
            send_sem=lon_send.at[rnd, j], recv_sem=lon_recv.at[rnd, j],
            device_id={"lat": li, "lon": lon_at(j)}, device_id_type=MESH)

    def red_lat_make(rnd, j, out):
        place = li if out else lax.rem(li - j + n_lat, n_lat)
        return pltpu.make_async_remote_copy(
            src_ref=red_lat.at[rnd, li], dst_ref=red_lat.at[rnd, place],
            send_sem=lat_send.at[rnd, j], recv_sem=lat_recv.at[rnd, j],
            device_id={"lat": lax.rem(li + j, n_lat), "lon": lo}, device_id_type=MESH)

    sums_row = lax.broadcasted_iota(jnp.int32, (8, clon), 0)

    def reduce_start(rnd, values):
        tile = jnp.zeros((8, clon), F32)
        for n, value in enumerate(values):
            tile = jnp.where(sums_row == n, value, tile)
        red_lon[rnd, lo] = tile
        for j in range(1, n_lon):
            red_lon_make(rnd, j, True).start()

    def reduce_turn(rnd):
        for j in range(1, n_lon):
            red_lon_make(rnd, j, False).wait_recv()
        red_lat[rnd, li] = jnp.sum(red_lon[rnd], axis=0)

        @pl.loop(1, n_lat)
        def _(j):
            red_lat_make(rnd, j, True).start()

    def reduce_end(rnd):
        @pl.loop(1, n_lat)
        def _(j):
            red_lat_make(rnd, j, False).wait_recv()
        return jnp.sum(red_lat[rnd], axis=0)

    def total(x):
        return jnp.sum(jnp.sum(x, axis=0, keepdims=True), axis=1, keepdims=True)

    def squares(x):
        return total(jnp.sum((x * x).reshape(-1, 8, clon), axis=0))

    def column_total(cols):
        return jnp.sum(sum(cols), axis=0, keepdims=True)

    recv_wide(term_make(0))
    apply_model(0, True)
    send_fetch(0)
    send_parts(0)
    bb_part = squares(parts_t[0])
    p1 = observe(0)
    u1 = [w_col[b] * p1[b] for b in range(cap)]
    spread(1, u1)
    reduce_start(0, [bb_part, column_total([u1[b] * p1[b] for b in range(cap)])])
    reduce_turn(0)
    recv_wide(term_make(1))
    apply_model(1, True)
    send_fetch(1)
    send_parts(1)
    sums = reduce_end(0)
    bb, s1 = sums[0:1, 0:1], sums[1:2, 0:1]
    alpha1 = bb / (bb + s1)
    left1 = s1 / (bb + s1)
    rr_part = squares(left1 * parts_t[0] - alpha1 * parts_t[1])
    g1 = observe(1)
    pr = [left1 * p1[b] - alpha1 * g1[b] for b in range(cap)]
    ur = [w_col[b] * pr[b] for b in range(cap)]
    spread(2, ur)
    reduce_start(1, [rr_part, column_total([ur[b] * pr[b] for b in range(cap)]),
                     column_total([ur[b] * p1[b] for b in range(cap)])])
    reduce_turn(1)
    recv_wide(term_make(2))
    apply_model(2, False)
    send_parts(2)
    sums = reduce_end(1)
    rr, srr, sr1 = sums[0:1, 0:1], sums[1:2, 0:1], sums[2:3, 0:1]
    beta = rr / bb
    curve = rr + beta * beta * bb + (srr + 2.0 * beta * sr1 + beta * beta * s1)
    alpha2 = rr / curve
    for rnd in range(3):
        for j in range(1, n_lon):
            part_make(rnd, j, False).wait_recv()

    for ref, value in ((alpha1_out, alpha1), (left1_out, left1), (alpha2_out, alpha2), (beta_out, beta)):
        ref[...] = jnp.broadcast_to(value, (1, clon)).reshape(1, 1, clon)

    done_wide(rate_make)
    done_wide(code_make)
    for rnd in range(3):
        done_wide(term_make(rnd))
        for j in range(1, n_lon):
            part_make(rnd, j, True).wait_send()
    for rnd in range(2):
        for j in range(1, n_lon):
            fetch_make(rnd, j, True).wait_send()
            red_lon_make(rnd, j, True).wait_send()

        @pl.loop(1, n_lat)
        def _(j, rnd=rnd):
            red_lat_make(rnd, j, True).wait_send()


def shards(n_lat, n_lon, courant, obs_matrix, obs_weight, innovation, block_owner, block_row, block_count):
    _, levels, clat, clon = courant.shape
    cap = block_row.shape[1]
    share = levels // n_lon
    ext = clat + 2 * HALO
    tile_rows = n_lon * ext
    unit = clon // cap
    src_pad = -(-3 * n_lon // unit) * unit
    vmem = pl.BlockSpec(memory_space=pltpu.VMEM)
    hbm = pl.BlockSpec(memory_space=pl.ANY)
    dma = pltpu.SemaphoreType.DMA
    scalar = jax.ShapeDtypeStruct((1, 1, clon), F32)
    parts, alpha1, left1, alpha2, beta = pl.pallas_call(
        functools.partial(kernel, n_lat, n_lon),
        out_shape=(
            jax.ShapeDtypeStruct((3, levels, clat, clon), F32),
            scalar, scalar, scalar, scalar,
        ),
        in_specs=[hbm] * 7,
        out_specs=(vmem,) * 5,
        scratch_shapes=[
            pltpu.VMEM((2, levels, clat, clon), F32),
            pltpu.VMEM((2, share, n_lon, ext, clon), F32),
            pltpu.VMEM((5, share, tile_rows, clon), F32),
            pltpu.VMEM((cap, clon, clon), F32),
            pltpu.VMEM((3, src_pad, cap, clon), F32),
            pltpu.VMEM((src_pad, cap, clon), F32),
            pltpu.VMEM((3, cap, clon), F32),
            pltpu.VMEM((share * tile_rows, src_pad * cap), BF16),
            pltpu.VMEM((n_lon * cap, share * tile_rows), BF16),
            pltpu.VMEM((share, tile_rows, clon), F32),
            pltpu.VMEM((share, tile_rows, clon), F32),
            pltpu.VMEM((3, n_lon, share, clat, clon), F32),
            pltpu.VMEM((2, n_lon, cap, clon), F32),
            pltpu.VMEM((2, n_lon, cap, clon), F32),
            pltpu.VMEM((2, n_lon, 8, clon), F32),
            pltpu.VMEM((2, n_lat, 8, clon), F32),
            dma, dma, dma,
            dma((5, 3, n_lon)), dma((5, 3, n_lon)),
            dma((2, n_lon)), dma((2, n_lon)),
            dma((3, n_lon)), dma((3, n_lon)),
            dma((2, n_lon)), dma((2, n_lon)),
            dma((2, n_lat)), dma((2, n_lat)),
            pltpu.VMEM((1, cap, clon), F32), pltpu.VMEM((1, cap, clon), F32),
            pltpu.SMEM((1, cap), jnp.int32), pltpu.SMEM((1, cap), jnp.int32),
            pltpu.SMEM((1, 1), jnp.int32),
            dma((5,)),
        ],
        compiler_params=pltpu.CompilerParams(collective_id=0, has_side_effects=True),
    )(courant, obs_matrix, obs_weight, innovation, block_owner[:, :, 0], block_row, block_count)
    b0, t1, tr = parts[0], parts[1], parts[2]
    r1 = left1 * b0 - alpha1 * t1
    increment = alpha1 * b0 + alpha2 * (r1 + beta * b0)
    residual = r1 - alpha2 * (r1 + tr + beta * (b0 + t1))
    return increment, residual


def solution(mesh):
    placed = (
        P(None, None, "lat", "lon"),
        P("lat", "lon", None, None),
        P("lat", "lon", None),
        P("lat", "lon", None),
        P("lat", "lon", None),
        P("lat", "lon"),
        P("lat", "lon"),
    )
    return jax.shard_map(
        functools.partial(shards, mesh.shape["lat"], mesh.shape["lon"]),
        mesh=mesh,
        in_specs=placed,
        out_specs=(P(None, "lat", "lon"), P(None, "lat", "lon")),
        check_vma=False,
    )
```

profile of v0, /device:TPU:0, one launch (start us, length us, event | category | flops | bytes accessed | tf_op | source)
XLA Modules:
  0.0 41.9 jit_solution(5525777113606704120)
XLA Ops:
  1.3 38.2 %shard_map.86 = (f32[3,16,16,128]{3,2,1,0:T(8,128)}, f32[1,1,128]{2,1,0:T(1,128)}, f32[1,1,128]{2,1,0:T(1,128)}, f32[1,1,128]{2,1,0:T(1,128)}, f32[1,1,128]{2,1,0:T(1,128)}) custom-call(f32[2,16,16,128]{3,2,1,0:T(8,128)} %courant.1, f32[1,8,128,128]{3,2,1,0:T(8,128)} %obs.1, f32[1,8,128]{2,1,0:T(8,128)} %weight_in.1, f32[1,8,128]{2,1,0:T(8,128)} %innov_in.1, ...), custom_call_target="tpu_custom_call" | custom-call | tf_op jit(solution)/shard_map/pallas_call | solution.py:427
  39.4 0.0 copy-start.3
  39.4 0.0 copy-start
  39.5 0.0 copy-start.1
  39.5 0.0 copy-start.2
  39.5 0.6 %copy-done.3 = f32[1,1,128]{2,1,0:T(1,128)S(1)} copy-done((f32[1,1,128]{2,1,0:T(1,128)S(1)}, f32[1,1,128]{2,1,0:T(1,128)}, u32[]{:S(2)}) %copy-start.3) | copy-done | bytes 536
  40.0 0.0 copy-done
  40.1 0.0 copy-done.1
  40.1 0.1 copy-done.2
  40.2 1.8 %fusion.2 = (f32[16,16,128]{2,1,0:T(8,128)}, f32[16,16,128]{2,1,0:T(8,128)}) fusion(f32[3,16,16,128]{3,2,1,0:T(8,128)} %get-tuple-element.8, f32[128]{0:T(128)S(1)} %bitcast.52, f32[128]{0:T(128)S(1)} %bitcast.50, f32[128]{0:T(128)S(1)} %bitcast.51, f32[128]{0:T(128)S(1)} %bitcast.49), kind=kLoop, calls=%fused_computation.3 | loop fusion | flops 458752 | bytes 657408 | tf_op jit(solution)/shard_map/sub | solution.py:468
Async XLA Ops:
  39.4 0.6 %copy-start.3 = (f32[1,1,128]{2,1,0:T(1,128)S(1)}, f32[1,1,128]{2,1,0:T(1,128)}, u32[]{:S(2)}) copy-start(f32[1,1,128]{2,1,0:T(1,128)} %get-tuple-element.11) | copy-start | bytes 1540
  39.4 0.6 %copy-start = (f32[1,1,128]{2,1,0:T(1,128)S(1)}, f32[1,1,128]{2,1,0:T(1,128)}, u32[]{:S(2)}) copy-start(f32[1,1,128]{2,1,0:T(1,128)} %get-tuple-element.7) | copy-start | bytes 1540
  39.5 0.6 %copy-start.1 = (f32[1,1,128]{2,1,0:T(1,128)S(1)}, f32[1,1,128]{2,1,0:T(1,128)}, u32[]{:S(2)}) copy-start(f32[1,1,128]{2,1,0:T(1,128)} %get-tuple-element.10) | copy-start | bytes 1540
  39.5 0.7 %copy-start.2 = (f32[1,1,128]{2,1,0:T(1,128)S(1)}, f32[1,1,128]{2,1,0:T(1,128)}, u32[]{:S(2)}) copy-start(f32[1,1,128]{2,1,0:T(1,128)} %get-tuple-element.9) | copy-start | bytes 1540
where the time goes:
time: 42.1 us; the launch traced here: 41.9 us
  Pallas kernels  38.2 us (91%)
  other arithmetic  1.79 us (4%)
  between operations  1.32 us (3%)
  local copies, waits for them, and re-layouts  0.68 us (2%)
    pallas_call x1, Pallas kernels, shards(): pl.pallas_call(functools.partial(kernel, n_lat, n_lon), out_shape=(jax.Sh...  38.2 us
    sub x1, other arithmetic, shards(): residual = r1 - alpha2 * (r1 + tr + beta * (b0 + t1))  1.79 us

commit v1 on v0

v1 whole, which is shorter than its diff:
```python
import functools

import jax
import jax.numpy as jnp
from jax import lax
from jax.experimental import pallas as pl
from jax.experimental.pallas import tpu as pltpu
from jax.sharding import PartitionSpec as P

STEPS = 4
HALO = 2 * STEPS
SLOT = 2
WIN = 2 * HALO + 1
PAD_WIN = WIN + 1
MESH = pl.DeviceIdType.MESH
F32 = jnp.float32
BF16 = jnp.bfloat16


def split3(x):
    hi = x.astype(BF16)
    rest = x - hi.astype(F32)
    mid = rest.astype(BF16)
    low = (rest - mid.astype(F32)).astype(BF16)
    return hi, mid, low


def dot3(onehot, x):
    total = None
    for part in split3(x):
        term = jnp.dot(onehot, part, preferred_element_type=F32)
        total = term if total is None else total + term
    return total


def split_rates(c0, c1):
    a, b = jnp.maximum(c0, 0.0), jnp.maximum(-c0, 0.0)
    e, f = jnp.maximum(c1, 0.0), jnp.maximum(-c1, 0.0)
    return a, b, e, f, 1.0 - a - b - e - f


def kernel(
    n_lat, n_lon,
    courant, obs, weight_in, innov_in, owner_in, row_in, count_in,
    inc_out, res_out,
    flow, obs_v, terms, codes, code_out, hot, dense_hot, field, dense_field,
    main_out, main_edge, strip_out, strip_edge, main_in, strip_in, side_in,
    win_rates, lat_out, lat_in, lon_out, lon_in, lat_halo, lon_halo, parts, red_lon, red_lat,
    ask_out, ask_in,
    obs_sem, flow_sem, wide_send, wide_recv, lat_send, lat_recv, lon_send, lon_recv,
    red_lon_send, red_lon_recv, red_lat_send, red_lat_recv,
    weight, innov, owner, row, count, input_sems,
):
    li = lax.axis_index("lat")
    lo = lax.axis_index("lon")
    _, levels, clat, clon = flow.shape
    cap = obs_v.shape[0]
    n_src = 3 * n_lon
    n_blocks = codes.shape[0] * cap
    span = 4 * clat
    half = levels // 2
    ring = clat + HALO
    width = clon // levels

    small = [
        pltpu.make_async_copy(src, dst, input_sems.at[n])
        for n, (src, dst) in enumerate((
            (owner_in, owner), (row_in, row), (count_in, count), (weight_in, weight), (innov_in, innov)))
    ]
    for copy in small:
        copy.start()
    flow_copy = pltpu.make_async_copy(courant, flow, flow_sem)
    flow_copy.start()
    obs_copy = pltpu.make_async_copy(obs.at[0], obs_v, obs_sem)
    obs_copy.start()

    def exists(d):
        return (li + d >= 0) & (li + d < n_lat)

    def guarded(d, run):
        if d == 0:
            run()
        else:
            pl.when(exists(d))(run)

    def lon_at(j):
        return lax.rem(lo + j + n_lon, n_lon)

    barrier = pltpu.get_barrier_semaphore()

    def greet(lat, lon):
        pl.semaphore_signal(barrier, inc=1, device_id={"lat": lat, "lon": lon}, device_id_type=MESH)

    @pl.loop(1, n_lat)
    def _(j):
        greet(lax.rem(li + j, n_lat), lo)

    for d in (-1, 1):
        def hello(d=d):
            for j in range(1, n_lon):
                greet(li + d, lon_at(j))
        guarded(d, hello)
    for j in range(1, n_lon):
        greet(li, lon_at(j))

    for copy in small:
        copy.wait()

    sub = lax.broadcasted_iota(jnp.int32, (cap, clon), 0)
    live = count[0, 0]
    owners = [owner[0, b] for b in range(cap)]
    levs = [lax.div(row[0, b], jnp.int32(clat)) for b in range(cap)]
    lats = [row[0, b] - levs[b] * clat for b in range(cap)]
    slots = []
    for b in range(cap):
        s = jnp.int32(0)
        for c in range(b):
            s = s + (owners[c] == owners[b]).astype(jnp.int32)
        slots.append(jnp.minimum(s, SLOT - 1))
    for o in range(n_lon):
        for s in range(SLOT):
            lev = jnp.int32(0)
            for b in range(cap):
                lev = jnp.where((owners[b] == o) & (slots[b] == s), levs[b], lev)
            ask_out[0, o * SLOT + s] = lev

    def column(values):
        tile = jnp.full((cap, clon), values[0], jnp.int32)
        for b in range(1, cap):
            tile = jnp.where(sub == b, values[b], tile)
        return tile

    level_tile, lat_tile, owner_tile = column(levs), column(lats), column(owners)

    def code_of(owner_now, lat_now):
        return (level_tile * n_lon + owner_now) * span + lat_now + clat

    for d in (-1, 0, 1):
        code_out[d + 1] = jnp.where(sub < live, code_of(owner_tile, lat_tile - clat * d), -1).astype(F32)

    sides = (li > 0).astype(jnp.int32) + (li < n_lat - 1).astype(jnp.int32)
    pl.semaphore_wait(barrier, (n_lon - 1) + (n_lat - 1) + sides * (n_lon - 1))

    def wide(kind, d, j, src, dst):
        return pltpu.make_async_remote_copy(
            src_ref=src, dst_ref=dst,
            send_sem=wide_send.at[kind, d + 1, j], recv_sem=wide_recv.at[kind, d + 1, j],
            device_id={"lat": li + d, "lon": lon_at(j)}, device_id_type=MESH,
        )

    def slot_of(d, j, out):
        return (1 - d) * n_lon + (lo if out else lon_at(-j))

    def start_wide(make):
        for d in (-1, 1, 0):
            def run(d=d):
                for j in range(n_lon):
                    if (d, j) != (0, 0):
                        make(d, j, True).start()
            guarded(d, run)

    def recv_wide(make):
        for d in (-1, 1, 0):
            def run(d=d):
                for j in range(n_lon):
                    if (d, j) != (0, 0):
                        make(d, j, False).wait_recv()
            guarded(-d, run)

    def done_wide(make):
        for d in (-1, 1, 0):
            def run(d=d):
                for j in range(n_lon):
                    if (d, j) != (0, 0):
                        make(d, j, True).wait_send()
            guarded(d, run)

    def code_make(d, j, out):
        return wide(0, d, j, code_out.at[d + 1], codes.at[slot_of(d, j, out)])

    def ask_make(d, j, out):
        return wide(1, d, j, ask_out, ask_in.at[slot_of(d, j, out)])

    def place(d):
        return (HALO, clat) if d == 0 else ((0, HALO) if d == 1 else (HALO + clat, HALO))

    def main_make(d, j, out):
        first, size = place(d)
        src = main_out.at[j] if d == 0 else main_edge.at[(d + 1) // 2, j]
        return wide(2, d, j, src, main_in.at[:, lo if out else lon_at(-j), :, pl.ds(first, size), :])

    def strip_make(d, j, out):
        first, size = place(d)
        src = strip_out.at[j] if d == 0 else strip_edge.at[(d + 1) // 2, j]
        return wide(3, d, j, src, strip_in.at[lo if out else lon_at(-j), pl.ds(first, size), :])

    def term_make(rnd):
        def make(d, j, out):
            return wide(4 + rnd, d, j, terms.at[rnd, n_lon + lo], terms.at[rnd, slot_of(d, j, out)])
        return make

    def lat_make(d):
        return pltpu.make_async_remote_copy(
            src_ref=lat_out.at[(d + 1) // 2], dst_ref=lat_in.at[(1 - d) // 2],
            send_sem=lat_send.at[(d + 1) // 2], recv_sem=lat_recv.at[(d + 1) // 2],
            device_id={"lat": li + d, "lon": lo}, device_id_type=MESH)

    def lon_make(role, d):
        if d == 0:
            first, size, dst = 0, clat, 0
        elif d == 1:
            first, size, dst = clat - HALO, HALO, clat + HALO
        else:
            first, size, dst = 0, HALO, clat
        return pltpu.make_async_remote_copy(
            src_ref=lon_out.at[role, :, pl.ds(first, size), :], dst_ref=lon_in.at[role, :, pl.ds(dst, size), :],
            send_sem=lon_send.at[role, d + 1], recv_sem=lon_recv.at[role, d + 1],
            device_id={"lat": li + d, "lon": lon_at(-1 if role == 0 else 1)}, device_id_type=MESH)

    start_wide(ask_make)
    start_wide(code_make)
    codes[n_lon + lo] = code_out[1]

    low = sub[:HALO] < STEPS
    flow_copy.wait()
    for f in range(2):
        for n in range(half):
            lat_out[1, f, n] = jnp.where(
                low, pltpu.roll(flow[f, n + half, clat - HALO:clat, :], STEPS, 0), flow[f, n, clat - HALO:clat, :])
            lat_out[0, f, n] = jnp.where(
                low, flow[f, n, 0:HALO, :], pltpu.roll(flow[f, n + half, 0:HALO, :], STEPS, 0))
    for d in (-1, 1):
        def send_lat(d=d):
            lat_make(d).start()
        guarded(d, send_lat)

    live_rows = sub < live
    w_rows = jnp.where(live_rows, weight[0], 0.0)
    wy_rows = w_rows * innov[0]
    stacked = jnp.concatenate([w_rows, wy_rows, jnp.zeros((clon - 2 * cap, clon), F32)], axis=0)
    columns = jnp.transpose(stacked)
    w_col = [columns[:, b:b + 1] for b in range(cap)]
    wy_col = [columns[:, cap + b:cap + b + 1] for b in range(cap)]

    def spread(rnd, u_cols):
        out = [jnp.sum(obs_v[b] * u_cols[b], axis=0, keepdims=True) for b in range(cap)]
        terms[rnd, n_lon + lo] = jnp.concatenate(out, axis=0)
        start_wide(term_make(rnd))

    obs_copy.wait()
    spread(0, wy_col)

    lane = lax.broadcasted_iota(jnp.int32, (1, clon), 1)
    group = lane // HALO

    def answer(d, j):
        if d == 0:
            first, size = 0, clat
        elif d == 1:
            first, size = clat - HALO, HALO
        else:
            first, size = 0, HALO
        slot = (d + 1) * n_lon + lon_at(j)

        def asked(o, s):
            if (d, j) == (0, 0):
                return ask_out[0, o * SLOT + s]
            return ask_in[slot, 0, o * SLOT + s]

        tile = jnp.zeros((size, clon), F32)
        for s in range(SLOT):
            lev = asked(lo, s)
            right, left = asked(lon_at(-1), s), asked(lon_at(1), s)
            for f in range(2):
                rows = flow[f, lev, first:first + size, :]
                if (d, j) == (0, 0):
                    main_in[f, lo, s, HALO:HALO + clat, :] = rows
                elif d == 0:
                    main_out[j, f, s] = rows
                else:
                    main_edge[(d + 1) // 2, j, f, s] = rows
                g = s * 2 + f
                moved = pltpu.roll(flow[f, right, first:first + size, :], g * HALO, 1)
                tile = jnp.where(group == g, moved, tile)
                g = (SLOT + s) * 2 + f
                moved = pltpu.roll(flow[f, left, first:first + size, :], (g + 1) * HALO, 1)
                tile = jnp.where(group == g, moved, tile)
        if (d, j) == (0, 0):
            strip_in[lo, HALO:HALO + clat, :] = tile
        else:
            if d == 0:
                strip_out[j] = tile
            else:
                strip_edge[(d + 1) // 2, j] = tile
            main_make(d, j, True).start()
            strip_make(d, j, True).start()

    recv_wide(ask_make)
    for d in (-1, 1, 0):
        def respond(d=d):
            for j in range(n_lon):
                if (d, j) != (0, 0):
                    answer(d, j)
        guarded(d, respond)
    answer(0, 0)

    lane_level = lane // width
    for f in range(2):
        right = jnp.zeros((clat, clon), F32)
        left = jnp.zeros((clat, clon), F32)
        for n in range(levels):
            rows = flow[f, n]
            right = jnp.where(lane_level == n, pltpu.roll(rows, n * width, 1), right)
            left = jnp.where(lane_level == n, pltpu.roll(rows, (n * width + width) % clon, 1), left)
        lon_out[0, f] = right
        lon_out[1, f] = left
    for d in (-1, 1, 0):
        def send_lon(d=d):
            for role in range(2):
                lon_make(role, d).start()
        guarded(d, send_lon)

    pad = codes.shape[0] - n_src
    none = jnp.full((n_lon, cap, clon), -1.0, F32)
    if pad:
        codes[n_src:] = jnp.full((pad, cap, clon), -1.0, F32)
        for rnd in range(3):
            terms[rnd, n_src:] = jnp.zeros((pad, cap, clon), F32)
    for d in (-1, 1):
        @pl.when(jnp.logical_not(exists(d)))
        def _(d=d):
            first = (d + 1) * n_lon
            codes[first:first + n_lon] = none
            for rnd in range(3):
                terms[rnd, first:first + n_lon] = jnp.zeros((n_lon, cap, clon), F32)
            lat0 = 0 if d == -1 else HALO + clat
            main_in[:, :, :, lat0:lat0 + HALO, :] = jnp.zeros((2, n_lon, SLOT, HALO, clon), F32)
            strip_in[:, lat0:lat0 + HALO, :] = jnp.zeros((n_lon, HALO, clon), F32)
            lat_in[(d + 1) // 2] = jnp.zeros((2, half, HALO, clon), F32)
            lon0 = clat + HALO if d == -1 else clat
            lon_in[:, :, lon0:lon0 + HALO, :] = jnp.zeros((2, 2, HALO, clon), F32)

    recv_wide(code_make)
    code_row = jnp.transpose(codes[...].reshape(n_blocks, clon))[0:1, :]

    def wide_tile(tile):
        return jnp.concatenate([tile] * (n_blocks // clon), axis=1) if n_blocks > clon else tile[:, :n_blocks]

    def matches(place_code):
        return jnp.where(place_code.astype(F32) == code_row, 1.0, 0.0).astype(BF16)

    window_rows = PAD_WIN * cap
    for part, shift in enumerate((0, n_lon - 1, 1)):
        tile = wide_tile(code_of(lax.rem(owner_tile + shift, n_lon), lat_tile))
        for d in range(0, PAD_WIN, 2):
            first = part * window_rows + d * cap
            hot[first:first + 2 * cap, :] = matches(jnp.concatenate([tile + (d - HALO), tile + (d + 1 - HALO)], axis=0))
    ring_row = lax.broadcasted_iota(jnp.int32, (ring, n_blocks), 0)
    ring_lat = jnp.where(ring_row < clat + STEPS, ring_row, ring_row - ring) + clat
    for part, shift in enumerate((0, n_lon - 1, 1)):
        lon_now = lon_at(shift)
        for n in range(0, levels, 2):
            pair = [ring_lat + ((n + k) * n_lon + lon_now) * span for k in range(2)]
            first = (part * levels + n) * ring
            dense_hot[first:first + 2 * ring, :] = matches(jnp.concatenate(pair, axis=0))

    middle = clon // 2
    last_lane = lane == clon - 1
    first_lane = lane == 0

    def lon_up(m, s):
        mr, sr = pltpu.roll(m, clon - 1, 1), pltpu.roll(s, clon - 1, 1)
        return jnp.where(last_lane, sr, mr), jnp.where(last_lane, mr, sr)

    def lon_down(m, s):
        mr, sr = pltpu.roll(m, 1, 1), pltpu.roll(s, 1, 1)
        return jnp.where(first_lane, sr, mr), jnp.where(first_lane, mr, sr)

    def load_window(rnd):
        field[...] = dot3(hot[...], terms[rnd].reshape(n_blocks, clon))

    recv_wide(term_make(0))
    load_window(0)

    recv_wide(strip_make)
    for o in range(n_lon):
        from_right, from_left = strip_in[(o + 1) % n_lon], strip_in[(o - 1) % n_lon]
        for s in range(SLOT):
            for f in range(2):
                g = s * 2 + f
                right = pltpu.roll(from_right, (clon - g * HALO) % clon, 1)
                g = (SLOT + s) * 2 + f
                left = pltpu.roll(from_left, (2 * clon - HALO - g * HALO) % clon, 1)
                side_in[f, o, s] = jnp.where(lane < middle, right, left)
    recv_wide(main_make)

    def gather(ref, f, d):
        tile = None
        for b in range(cap):
            line = ref[f, owners[b], slots[b], pl.ds(lats[b] + d, 1), :]
            tile = jnp.broadcast_to(line, (cap, clon)) if tile is None else jnp.where(sub == b, line, tile)
        return tile

    for d in range(WIN):
        for side, ref in enumerate((main_in, side_in)):
            if d in (0, WIN - 1):
                if side == 0:
                    c0 = gather(ref, 0, d)
                    win_rates[1 if d == 0 else 0, d, side] = jnp.maximum(-c0 if d == 0 else c0, 0.0)
                continue
            for k, value in enumerate(split_rates(gather(ref, 0, d), gather(ref, 1, d))):
                win_rates[k, d, side] = value

    def window_model():
        a, b, e, f, keep = range(5)

        def part(n, d):
            first = n * window_rows + d * cap
            return field[first:first + cap, :]

        main = {d: part(0, d) for d in range(WIN)}
        side = {d: jnp.where(lane < middle, part(2, d), part(1, d)) for d in range(1, WIN - 1)}
        for step in range(STEPS):
            a_main = {d: win_rates[a, d, 0] * main[d] for d in range(step + 2, WIN - step)}
            b_main = {d: win_rates[b, d, 0] * main[d] for d in range(step, WIN - step - 2)}
            a_side = {d: win_rates[a, d, 1] * side[d] for d in range(step + 3, WIN - step - 1)}
            b_side = {d: win_rates[b, d, 1] * side[d] for d in range(step + 1, WIN - step - 3)}
            new_main, new_side = {}, {}
            for d in range(step + 1, WIN - step - 1):
                up = lon_up(win_rates[e, d, 0] * main[d], win_rates[e, d, 1] * side[d])
                down = lon_down(win_rates[f, d, 0] * main[d], win_rates[f, d, 1] * side[d])
                new_main[d] = win_rates[keep, d, 0] * main[d] + a_main[d + 1] + b_main[d - 1] + up[0] + down[0]
                if step + 2 <= d < WIN - step - 2:
                    new_side[d] = win_rates[keep, d, 1] * side[d] + a_side[d + 1] + b_side[d - 1] + up[1] + down[1]
            main, side = new_main, new_side
        for d in list(main):
            lat_now = lat_tile + (li * clat + d - HALO)
            inside = (lat_now >= 0) & (lat_now < n_lat * clat)
            main[d] = jnp.where(inside, main[d], 0.0)
            if d in side:
                side[d] = jnp.where(inside, side[d], 0.0)
        for step in range(STEPS):
            reach = STEPS - 1 - step
            new_main, new_side = {}, {}
            for d in range(HALO - reach, HALO + reach + 1):
                down, up = lon_down(main[d], side[d]), lon_up(main[d], side[d])
                new_main[d] = (win_rates[keep, d, 0] * main[d] + win_rates[a, d, 0] * main[d - 1] + win_rates[b, d, 0] * main[d + 1]
                               + win_rates[e, d, 0] * down[0] + win_rates[f, d, 0] * up[0])
                if abs(d - HALO) < reach:
                    new_side[d] = (win_rates[keep, d, 1] * side[d] + win_rates[a, d, 1] * side[d - 1]
                                   + win_rates[b, d, 1] * side[d + 1] + win_rates[e, d, 1] * down[1] + win_rates[f, d, 1] * up[1])
            main, side = new_main, new_side
        seen = main[HALO]
        return [jnp.sum(obs_v[b] * seen[b:b + 1, :], axis=1, keepdims=True) for b in range(cap)]

    def recv_dense():
        for d in (-1, 1):
            def wait_lat(d=d):
                lat_make(d).wait_recv()
            guarded(-d, wait_lat)
        for d in (-1, 1, 0):
            def wait_lon(d=d):
                for role in range(2):
                    lon_make(role, d).wait_recv()
            guarded(-d, wait_lon)
        for f in range(2):
            for n in range(half):
                north, south = lat_in[1, f, n], lat_in[0, f, n]
                lat_halo[f, n] = jnp.where(low, north, south)
                lat_halo[f, n + half] = pltpu.roll(jnp.where(low, south, north), STEPS, 0)
            sides_in = []
            for role in range(2):
                edge = jnp.where(low, lon_in[role, f, clat:clat + HALO, :], lon_in[role, f, clat + HALO:, :])
                sides_in.append(jnp.concatenate([lon_in[role, f, 0:clat, :], edge], axis=0))
            for n in range(levels):
                right = pltpu.roll(sides_in[0], (clon - n * width) % clon, 1)
                left = pltpu.roll(sides_in[1], (2 * clon - width - n * width) % clon, 1)
                lon_halo[f, n] = jnp.where(lane < middle, right, left)

    def dense(rnd):
        flat = dot3(dense_hot[...], terms[rnd].reshape(n_blocks, clon))
        dense_field[...] = flat.reshape(3, levels, ring, clon)

        @pl.loop(0, levels, unroll=2)
        def _(n):
            rates = []
            for f in range(2):
                rates.append((jnp.concatenate([flow[f, n], lat_halo[f, n]], axis=0), lon_halo[f, n]))
            main_rates = split_rates(rates[0][0], rates[1][0])
            side_rates = split_rates(rates[0][1], rates[1][1])
            m = dense_field[0, n]
            s = jnp.where(lane < middle, dense_field[2, n], dense_field[1, n])
            for _ in range(STEPS):
                up = lon_up(main_rates[2] * m, side_rates[2] * s)
                down = lon_down(main_rates[3] * m, side_rates[3] * s)
                m, s = (
                    (r[4] * x + pltpu.roll(r[0] * x, ring - 1, 0) + pltpu.roll(r[1] * x, 1, 0) + up[k] + down[k])
                    for k, (r, x) in enumerate(((main_rates, m), (side_rates, s))))
            parts[rnd, n] = m[0:clat]

    def red_lon_make(j, out):
        return pltpu.make_async_remote_copy(
            src_ref=red_lon.at[lo], dst_ref=red_lon.at[lo if out else lon_at(-j)],
            send_sem=red_lon_send.at[j], recv_sem=red_lon_recv.at[j],
            device_id={"lat": li, "lon": lon_at(j)}, device_id_type=MESH)

    def red_lat_make(j, out):
        at = li if out else lax.rem(li - j + n_lat, n_lat)
        return pltpu.make_async_remote_copy(
            src_ref=red_lat.at[li], dst_ref=red_lat.at[at],
            send_sem=red_lat_send.at[j], recv_sem=red_lat_recv.at[j],
            device_id={"lat": lax.rem(li + j, n_lat), "lon": lo}, device_id_type=MESH)

    def column_total(xs, ys):
        return jnp.sum(sum(x * y for x, y in zip(xs, ys)), axis=0, keepdims=True)

    p1 = window_model()
    u1 = [w_col[b] * p1[b] for b in range(cap)]
    spread(1, u1)
    recv_dense()
    dense(0)
    recv_wide(term_make(1))
    load_window(1)
    g1 = window_model()
    u2 = [w_col[b] * g1[b] for b in range(cap)]
    tile = jnp.zeros((8, clon), F32)
    for n, value in enumerate((column_total(wy_col, p1), column_total(u1, p1), column_total(u1, g1), column_total(u2, g1))):
        tile = jnp.where(sub == n, value, tile)
    red_lon[lo] = tile
    for j in range(1, n_lon):
        red_lon_make(j, True).start()
    spread(2, u2)
    dense(1)
    for j in range(1, n_lon):
        red_lon_make(j, False).wait_recv()
    red_lat[li] = jnp.sum(red_lon[...], axis=0)

    @pl.loop(1, n_lat)
    def _(j):
        red_lat_make(j, True).start()

    recv_wide(term_make(2))
    dense(2)

    @pl.loop(1, n_lat)
    def _(j):
        red_lat_make(j, False).wait_recv()

    sums = jnp.sum(red_lat[...], axis=0)
    bb, s1, tt, s3 = (sums[n:n + 1, 0:1] for n in range(4))
    scale = bb + s1
    alpha1, left1 = bb / scale, s1 / scale
    rr = left1 * (left1 * bb - alpha1 * s1) - alpha1 * (left1 * s1 - alpha1 * tt)
    sr1 = left1 * s1 - alpha1 * tt
    srr = left1 * sr1 - alpha1 * (left1 * tt - alpha1 * s3)
    beta = rr / bb
    curve = rr + beta * beta * bb + (srr + 2.0 * beta * sr1 + beta * beta * s1)
    alpha2 = rr / curve
    mix = left1 + beta
    inc_b, inc_t = alpha1 + alpha2 * mix, -alpha2 * alpha1
    res_b, res_t, res_2 = left1 - alpha2 * mix, -alpha1 - alpha2 * (mix - alpha1), alpha2 * alpha1
    for n in range(levels):
        b0, t1, t2 = parts[0, n], parts[1, n], parts[2, n]
        inc_out[n] = inc_b * b0 + inc_t * t1
        res_out[n] = res_b * b0 + res_t * t1 + res_2 * t2

    for make in (code_make, ask_make, main_make, strip_make, term_make(0), term_make(1), term_make(2)):
        done_wide(make)
    for d in (-1, 1):
        def sent_lat(d=d):
            lat_make(d).wait_send()
        guarded(d, sent_lat)
    for d in (-1, 1, 0):
        def sent_lon(d=d):
            for role in range(2):
                lon_make(role, d).wait_send()
        guarded(d, sent_lon)
    for j in range(1, n_lon):
        red_lon_make(j, True).wait_send()

    @pl.loop(1, n_lat)
    def _(j):
        red_lat_make(j, True).wait_send()


def shards(n_lat, n_lon, courant, obs_matrix, obs_weight, innovation, block_owner, block_row, block_count):
    _, levels, clat, clon = courant.shape
    cap = block_row.shape[1]
    ring = clat + HALO
    rows = clat + 2 * HALO
    unit = clon // cap
    src_pad = -(-3 * n_lon // unit) * unit
    n_blocks = src_pad * cap
    vmem = pl.BlockSpec(memory_space=pltpu.VMEM)
    hbm = pl.BlockSpec(memory_space=pl.ANY)
    dma = pltpu.SemaphoreType.DMA

    def f32(*shape):
        return pltpu.VMEM(shape, F32)

    def i32(*shape):
        return pltpu.SMEM(shape, jnp.int32)

    field = jax.ShapeDtypeStruct((levels, clat, clon), F32)
    return pl.pallas_call(
        functools.partial(kernel, n_lat, n_lon),
        out_shape=(field, field),
        in_specs=[hbm] * 7,
        out_specs=(vmem, vmem),
        scratch_shapes=[
            f32(2, levels, clat, clon),
            f32(cap, clon, clon),
            f32(3, src_pad, cap, clon),
            f32(src_pad, cap, clon),
            f32(3, cap, clon),
            pltpu.VMEM((3 * PAD_WIN * cap, n_blocks), BF16),
            pltpu.VMEM((3 * levels * ring, n_blocks), BF16),
            f32(3 * PAD_WIN * cap, clon),
            f32(3, levels, ring, clon),
            f32(n_lon, 2, SLOT, clat, clon),
            f32(2, n_lon, 2, SLOT, HALO, clon),
            f32(n_lon, clat, clon),
            f32(2, n_lon, HALO, clon),
            f32(2, n_lon, SLOT, rows, clon),
            f32(n_lon, rows, clon),
            f32(2, n_lon, SLOT, rows, clon),
            f32(5, WIN, 2, cap, clon),
            f32(2, 2, levels // 2, HALO, clon),
            f32(2, 2, levels // 2, HALO, clon),
            f32(2, 2, clat, clon),
            f32(2, 2, rows, clon),
            f32(2, levels, HALO, clon),
            f32(2, levels, ring, clon),
            f32(3, levels, clat, clon),
            f32(n_lon, 8, clon),
            f32(n_lat, 8, clon),
            i32(1, n_lon * SLOT),
            i32(3 * n_lon, 1, n_lon * SLOT),
            dma, dma,
            dma((7, 3, n_lon)), dma((7, 3, n_lon)),
            dma((2,)), dma((2,)),
            dma((2, 3)), dma((2, 3)),
            dma((n_lon,)), dma((n_lon,)),
            dma((n_lat,)), dma((n_lat,)),
            f32(1, cap, clon), f32(1, cap, clon),
            i32(1, cap), i32(1, cap), i32(1, 1),
            dma((5,)),
        ],
        compiler_params=pltpu.CompilerParams(collective_id=0, has_side_effects=True),
    )(courant, obs_matrix, obs_weight, innovation, block_owner[:, :, 0], block_row, block_count)


def solution(mesh):
    placed = (
        P(None, None, "lat", "lon"),
        P("lat", "lon", None, None),
        P("lat", "lon", None),
        P("lat", "lon", None),
        P("lat", "lon", None),
        P("lat", "lon"),
        P("lat", "lon"),
    )
    return jax.shard_map(
        functools.partial(shards, mesh.shape["lat"], mesh.shape["lon"]),
        mesh=mesh,
        in_specs=placed,
        out_specs=(P(None, "lat", "lon"), P(None, "lat", "lon")),
        check_vma=False,
    )
```

time: 42.1 us -> 36.8 us (0.87)
  Pallas kernels: 38.2 us -> 33.1 us
  other arithmetic: 1.79 us -> 0 us
  local copies, waits for them, and re-layouts: 0.68 us -> 2.26 us
    pallas_call x1, Pallas kernels: 38.2 us -> 33.1 us  [shards(): pl.pallas_call(functools.partial(kernel, n_lat, n_lon), out_shape=(field,...]
    sub x1 -> x0, other arithmetic: 1.79 us -> none  [shards(): residual = r1 - alpha2 * (r1 + tr + beta * (b0 + t1))]
    unnamed x8 -> x4, local copies, waits for them, and re-layouts: 0.68 us -> 2.26 us
where the time goes in v1:
time: 36.8 us; the launch traced here: 36.6 us
  Pallas kernels  33.1 us (90%)
  local copies, waits for them, and re-layouts  2.26 us (6%)
  between operations  1.3 us (4%)
    pallas_call x1, Pallas kernels, shards(): pl.pallas_call(functools.partial(kernel, n_lat, n_lon), out_shape=(field,...  33.1 us
    unnamed x4, local copies, waits for them, and re-layouts  2.26 us

profile of v1, /device:TPU:0, one launch (start us, length us, event | category | flops | bytes accessed | tf_op | source)
XLA Modules:
  0.0 36.6 jit_solution(6365729352145494128)
XLA Ops:
  1.3 33.1 %shard_map.86 = (f32[16,16,128]{2,1,0:T(8,128)}, f32[16,16,128]{2,1,0:T(8,128)}) custom-call(f32[2,16,16,128]{3,2,1,0:T(8,128)} %courant.1, f32[1,8,128,128]{3,2,1,0:T(8,128)} %obs.1, f32[1,8,128]{2,1,0:T(8,128)} %weight_in.1, f32[1,8,128]{2,1,0:T(8,128)} %innov_in.1, s32[1,8]{1,0:T(1,128)} %bitcast.1, s32[1,8]{1,0:T(1,128)} %row_in.1, s32[1,1]{1,0:T(1,128)S(6)} %copy.11.count_in), custom_call_target="tpu_custom_call" | custom-call | tf_op jit(solution)/shard_map/pallas_call | solution.py:605
  34.4 0.0 copy-start
  34.4 1.6 %copy.12 = f32[16,16,128]{2,1,0:T(8,128)} copy(f32[16,16,128]{2,1,0:T(8,128)} %get-tuple-element.4) | data formatting | bytes 262144
  36.0 0.0 copy-done
  36.0 0.7 %copy.13 = f32[16,16,128]{2,1,0:T(8,128)} copy(f32[16,16,128]{2,1,0:T(8,128)S(1)} %copy-done) | data formatting | bytes 262144
Async XLA Ops:
  34.4 1.6 %copy-start = (f32[16,16,128]{2,1,0:T(8,128)S(1)}, f32[16,16,128]{2,1,0:T(8,128)}, u32[]{:S(2)}) copy-start(f32[16,16,128]{2,1,0:T(8,128)} %get-tuple-element.5) | copy-start | bytes 393220

commit v2 on v1

v2 whole, which is shorter than its diff:
```python
import functools

import jax
import jax.numpy as jnp
from jax import lax
from jax.experimental import pallas as pl
from jax.experimental.pallas import tpu as pltpu
from jax.sharding import PartitionSpec as P

STEPS = 4
HALO = 2 * STEPS
SLOT = 2
WIN = 2 * HALO + 1
PAD_WIN = WIN + 1
MESH = pl.DeviceIdType.MESH
F32 = jnp.float32
BF16 = jnp.bfloat16


def split3(x):
    hi = x.astype(BF16)
    rest = x - hi.astype(F32)
    mid = rest.astype(BF16)
    low = (rest - mid.astype(F32)).astype(BF16)
    return hi, mid, low


def dot3(onehot, parts):
    total = None
    for part in parts:
        term = jnp.dot(onehot, part, preferred_element_type=F32)
        total = term if total is None else total + term
    return total


def split_rates(c0, c1):
    a, b = jnp.maximum(c0, 0.0), jnp.maximum(-c0, 0.0)
    e, f = jnp.maximum(c1, 0.0), jnp.maximum(-c1, 0.0)
    return a, b, e, f, 1.0 - a - b - e - f


def kernel(
    n_lat, n_lon,
    courant, courant_flat, obs, weight_in, innov_in, owner_in, row_in, count_in,
    inc_out, res_out,
    flow, flow_flat, obs_v, terms, codes, code_out, hot_main, hot_side, dense_main, dense_side, field, dense_field,
    main_out, main_edge, strip_out, strip_edge, main_in, strip_in, side_in,
    win_rates, lat_out, lat_in, lon_out, lon_in, dense_rates, weight_wide, parts, red_lon, red_lat,
    ask_out, ask_in,
    obs_sem, flow_sem, flat_sem, wide_send, wide_recv, lat_send, lat_recv, lon_send, lon_recv, red_sems,
    weight, innov, owner, row, count, input_sems,
):
    li = lax.axis_index("lat")
    lo = lax.axis_index("lon")
    clon = flow_flat.shape[1]
    cap = obs_v.shape[0]
    tiles, clat = parts.shape[1:3]
    levels = tiles * 8
    n_src = 3 * n_lon
    n_blocks = terms.shape[1] * cap
    span = 4 * clat
    ring = clat + 2 * STEPS
    width = clon // clat

    small = [
        pltpu.make_async_copy(src, dst, input_sems.at[n])
        for n, (src, dst) in enumerate((
            (owner_in, owner), (row_in, row), (count_in, count), (weight_in, weight), (innov_in, innov)))
    ]
    for copy in small:
        copy.start()
    flow_copy = pltpu.make_async_copy(courant, flow, flow_sem)
    flow_copy.start()
    flat_copy = pltpu.make_async_copy(courant_flat, flow_flat, flat_sem)
    obs_copy = pltpu.make_async_copy(obs.at[0], obs_v, obs_sem)
    obs_copy.start()
    flat_copy.start()

    def exists(d):
        return (li + d >= 0) & (li + d < n_lat)

    def guarded(d, run):
        if d == 0:
            run()
        else:
            pl.when(exists(d))(run)

    def lon_at(j):
        return lax.rem(lo + j + n_lon, n_lon)

    barrier = pltpu.get_barrier_semaphore()

    def greet(lat, lon):
        pl.semaphore_signal(barrier, inc=1, device_id={"lat": lat, "lon": lon}, device_id_type=MESH)

    @pl.loop(1, n_lat)
    def _(j):
        greet(lax.rem(li + j, n_lat), lo)

    for d in (-1, 1):
        def hello(d=d):
            for j in range(1, n_lon):
                greet(li + d, lon_at(j))
        guarded(d, hello)
    for j in range(1, n_lon):
        greet(li, lon_at(j))

    for copy in small:
        copy.wait()

    sub = lax.broadcasted_iota(jnp.int32, (cap, clon), 0)
    live = count[0, 0]
    owners = [owner[0, b] for b in range(cap)]
    levs = [lax.div(row[0, b], jnp.int32(clat)) for b in range(cap)]
    lats = [row[0, b] - levs[b] * clat for b in range(cap)]
    slots = []
    for b in range(cap):
        s = jnp.int32(0)
        for c in range(b):
            s = s + (owners[c] == owners[b]).astype(jnp.int32)
        slots.append(jnp.minimum(s, SLOT - 1))
    for o in range(n_lon):
        for s in range(SLOT):
            lev = jnp.int32(0)
            for b in range(cap):
                lev = jnp.where((owners[b] == o) & (slots[b] == s), levs[b], lev)
            ask_out[0, o * SLOT + s] = lev

    def column(values):
        tile = jnp.full((cap, clon), values[0], jnp.int32)
        for b in range(1, cap):
            tile = jnp.where(sub == b, values[b], tile)
        return tile

    level_tile, lat_tile, owner_tile = column(levs), column(lats), column(owners)

    def code_of(owner_now, lat_now):
        return (level_tile * n_lon + owner_now) * span + lat_now + clat

    lane = lax.broadcasted_iota(jnp.int32, (1, clon), 1)
    middle = clon // 2
    code_line = jnp.full((1, clon), -1, jnp.int32)
    for b in range(cap):
        code = (levs[b] * n_lon + owners[b]) * span + lats[b] + clat
        code_line = jnp.where(lane == b, jnp.where(b < live, code, -4 * span), code_line)
    for d in (-1, 0, 1):
        code_out[d + 1] = (code_line - clat * d).astype(F32)

    sides = (li > 0).astype(jnp.int32) + (li < n_lat - 1).astype(jnp.int32)
    pl.semaphore_wait(barrier, (n_lon - 1) + (n_lat - 1) + sides * (n_lon - 1))

    def wide(kind, d, j, src, dst):
        return pltpu.make_async_remote_copy(
            src_ref=src, dst_ref=dst,
            send_sem=wide_send.at[kind, d + 1], recv_sem=wide_recv.at[kind, d + 1],
            device_id={"lat": li + d, "lon": lon_at(j)}, device_id_type=MESH,
        )

    def slot_of(d, j, out):
        return (1 - d) * n_lon + (lo if out else lon_at(-j))

    def several(d):
        return n_lon - 1 if d == 0 else n_lon

    def start_wide(make):
        for d in (-1, 1, 0):
            def run(d=d):
                for j in (2, 3, 1, 0) if n_lon == 4 else range(n_lon):
                    if (d, j) != (0, 0):
                        make(d, j).start()
            guarded(d, run)

    def recv_wide(whole):
        for d in (-1, 1, 0):
            def run(d=d):
                kind, _, into = whole(d)
                wide(kind, d, 1, into, into).wait_recv()
            guarded(-d, run)

    def done_wide(whole):
        for d in (-1, 1, 0):
            def run(d=d):
                kind, out, _ = whole(d)
                wide(kind, d, 1, out, out).wait_send()
            guarded(d, run)

    def code_make(d, j):
        return wide(0, d, j, code_out.at[d + 1], codes.at[slot_of(d, j, True)])

    def code_all(d):
        ref = codes.at[pl.ds((1 - d) * n_lon, several(d))]
        return 0, ref, ref

    def ask_make(d, j):
        return wide(1, d, j, ask_out, ask_in.at[slot_of(d, j, True)])

    def ask_all(d):
        ref = ask_in.at[pl.ds((1 - d) * n_lon, several(d))]
        return 1, ref, ref

    def place(d):
        return (HALO, clat) if d == 0 else ((0, HALO) if d == 1 else (HALO + clat, HALO))

    def main_make(d, j):
        first, size = place(d)
        src = main_out.at[j] if d == 0 else main_edge.at[(d + 1) // 2, j]
        return wide(2, d, j, src, main_in.at[:, lo, :, pl.ds(first, size), :])

    def main_all(d):
        first, size = place(d)
        src = main_out.at[pl.ds(1, n_lon - 1)] if d == 0 else main_edge.at[(d + 1) // 2]
        return 2, src, main_in.at[:, pl.ds(0, several(d)), :, pl.ds(first, size), :]

    def strip_make(d, j):
        first, size = place(d)
        src = strip_out.at[j] if d == 0 else strip_edge.at[(d + 1) // 2, j]
        return wide(3, d, j, src, strip_in.at[lo, pl.ds(first, size), :])

    def strip_all(d):
        first, size = place(d)
        src = strip_out.at[pl.ds(1, n_lon - 1)] if d == 0 else strip_edge.at[(d + 1) // 2]
        return 3, src, strip_in.at[pl.ds(0, several(d)), pl.ds(first, size), :]

    def term_make(rnd):
        def make(d, j):
            return wide(4 + rnd, d, j, terms.at[rnd, n_lon + lo], terms.at[rnd, slot_of(d, j, True)])
        return make

    def term_all(rnd):
        def whole(d):
            ref = terms.at[rnd, pl.ds((1 - d) * n_lon, several(d))]
            return 4 + rnd, ref, ref
        return whole

    def lat_make(d):
        return pltpu.make_async_remote_copy(
            src_ref=lat_out.at[(d + 1) // 2], dst_ref=lat_in.at[(1 - d) // 2],
            send_sem=lat_send.at[(d + 1) // 2], recv_sem=lat_recv.at[(d + 1) // 2],
            device_id={"lat": li + d, "lon": lo}, device_id_type=MESH)

    def lon_make(role, d):
        return pltpu.make_async_remote_copy(
            src_ref=lon_out.at[role], dst_ref=lon_in.at[role, 1 - d],
            send_sem=lon_send.at[role, d + 1], recv_sem=lon_recv.at[role, d + 1],
            device_id={"lat": li + d, "lon": lon_at(-1 if role == 0 else 1)}, device_id_type=MESH)

    start_wide(ask_make)
    start_wide(code_make)
    codes[n_lon + lo] = code_out[1]

    flow_copy.wait()

    def flow_rows(f, lev, first, size):
        return flow[f, lev, first:first + size, :]

    def flow_levels(f, tile, lat):
        return flow_flat[pl.ds((f * levels + tile * 8) * clat + lat, 8, stride=clat), :]

    live_rows = sub < live
    w_rows = jnp.where(live_rows, weight[0], 0.0)
    wy_rows = w_rows * innov[0]
    stacked = jnp.concatenate([w_rows, wy_rows, jnp.zeros((clon - 2 * cap, clon), F32)], axis=0)
    columns = jnp.transpose(stacked)
    for b in range(cap):
        weight_wide[b] = jnp.broadcast_to(columns[:, b:b + 1], (clon, clon))
    wy_col = [columns[:, cap + b:cap + b + 1] for b in range(cap)]

    def spread(rnd, u_cols):
        out = [jnp.sum(obs_v[b] * u_cols[b], axis=0, keepdims=True) for b in range(cap)]
        terms[rnd, n_lon + lo] = jnp.concatenate(out, axis=0)
        start_wide(term_make(rnd))

    obs_copy.wait()
    spread(0, wy_col)

    group = lane // HALO

    def answer(d, j):
        if d == 0:
            first, size = 0, clat
        elif d == 1:
            first, size = clat - HALO, HALO
        else:
            first, size = 0, HALO
        slot = (d + 1) * n_lon + lon_at(j)

        def asked(o, s):
            if (d, j) == (0, 0):
                return ask_out[0, o * SLOT + s]
            return ask_in[slot, 0, o * SLOT + s]

        tile = jnp.zeros((size, clon), F32)
        for s in range(SLOT):
            lev = asked(lo, s)
            right, left = asked(lon_at(-1), s), asked(lon_at(1), s)
            for f in range(2):
                rows = flow_rows(f, lev, first, size)
                if (d, j) == (0, 0):
                    main_in[f, lo, s, HALO:HALO + clat, :] = rows
                elif d == 0:
                    main_out[j, f, s] = rows
                else:
                    main_edge[(d + 1) // 2, j, f, s] = rows
                g = s * 2 + f
                moved = pltpu.roll(flow_rows(f, right, first, size), g * HALO, 1)
                tile = jnp.where(group == g, moved, tile)
                g = (SLOT + s) * 2 + f
                moved = pltpu.roll(flow_rows(f, left, first, size), (g + 1) * HALO, 1)
                tile = jnp.where(group == g, moved, tile)
        if (d, j) == (0, 0):
            strip_in[lo, HALO:HALO + clat, :] = tile
        else:
            if d == 0:
                strip_out[j] = tile
            else:
                strip_edge[(d + 1) // 2, j] = tile
            main_make(d, j).start()
            strip_make(d, j).start()

    recv_wide(ask_all)
    for d in (-1, 1, 0):
        def respond(d=d):
            for j in range(n_lon):
                if (d, j) != (0, 0):
                    answer(d, j)
        guarded(d, respond)
    answer(0, 0)

    def send_dense():
        flat_copy.wait()
        for f in range(2):
            for t in range(tiles):
                for k in range(STEPS):
                    lat_out[0, f, k, t] = flow_levels(f, t, k)
                    lat_out[1, f, k, t] = flow_levels(f, t, clat - STEPS + k)
        for d in (-1, 1):
            def send_lat(d=d):
                lat_make(d).start()
            guarded(d, send_lat)
        lane_lat = lane // width
        for f in range(2):
            for t in range(tiles):
                right = jnp.zeros((8, clon), F32)
                left = jnp.zeros((8, clon), F32)
                for n in range(clat):
                    rows = flow_levels(f, t, n)
                    right = jnp.where(lane_lat == n, pltpu.roll(rows, n * width, 1), right)
                    left = jnp.where(lane_lat == n, pltpu.roll(rows, (n * width + width) % clon, 1), left)
                lon_out[0, f, t] = right
                lon_out[1, f, t] = left
        for d in (-1, 1, 0):
            def send_lon(d=d):
                for role in range(2):
                    lon_make(role, d).start()
            guarded(d, send_lon)

    pad = terms.shape[1] - n_src
    if pad:
        for rnd in range(3):
            terms[rnd, n_src:] = jnp.zeros((pad, cap, clon), F32)
    for d in (-1, 1):
        @pl.when(jnp.logical_not(exists(d)))
        def _(d=d):
            first = (d + 1) * n_lon
            codes[first:first + n_lon] = jnp.full((n_lon, 1, clon), -4.0 * span, F32)
            for rnd in range(3):
                terms[rnd, first:first + n_lon] = jnp.zeros((n_lon, cap, clon), F32)
            lat0 = 0 if d == -1 else HALO + clat
            main_in[:, :, :, lat0:lat0 + HALO, :] = jnp.zeros((2, n_lon, SLOT, HALO, clon), F32)
            strip_in[:, lat0:lat0 + HALO, :] = jnp.zeros((n_lon, HALO, clon), F32)
            lat_in[(d + 1) // 2] = jnp.zeros((2, STEPS, tiles, 8, clon), F32)
            lon_in[:, d + 1] = jnp.zeros((2, 2, tiles, 8, clon), F32)

    recv_wide(code_all)
    code_parts = []
    for first in range(0, n_blocks, clon):
        line = jnp.full((1, clon), -4.0 * span, F32)
        for k in range(clon // cap):
            slot = first // cap + k
            if slot < n_src:
                line = jnp.where(lane // cap == k, pltpu.roll(codes[slot], k * cap, 1), line)
        code_parts.append(line)
    code_row = code_parts[0] if len(code_parts) == 1 else jnp.concatenate(code_parts, axis=1)

    def wide_tile(tile):
        return jnp.concatenate([tile] * (n_blocks // clon), axis=1) if n_blocks > clon else tile[:, :n_blocks]

    def matches(place_code):
        return jnp.where(place_code.astype(F32) == code_row, 1.0, 0.0).astype(BF16)

    for part, shift in enumerate((0, n_lon - 1, 1)):
        tile = wide_tile(code_of(lax.rem(owner_tile + shift, n_lon), lat_tile))
        for d in range(0, PAD_WIN, 2):
            rows = matches(jnp.concatenate([tile + (d - HALO), tile + (d + 1 - HALO)], axis=0))
            if part == 0:
                hot_main[d * cap:(d + 2) * cap, :] = rows
            else:
                hot_side[d * cap:(d + 2) * cap, (part - 1) * n_blocks:part * n_blocks] = rows

    def build_dense():
        lev_codes = lax.broadcasted_iota(jnp.int32, (levels, n_blocks), 0) * (n_lon * span)
        for part, shift in enumerate((0, n_lon - 1, 1)):
            for d in range(ring):
                rows = matches(lev_codes + (lon_at(shift) * span + (d - STEPS + clat)))
                if part == 0:
                    dense_main[d * levels:(d + 1) * levels, :] = rows
                else:
                    dense_side[d * levels:(d + 1) * levels, (part - 1) * n_blocks:part * n_blocks] = rows

    last_lane = lane == clon - 1
    first_lane = lane == 0

    def lon_up(m, s):
        mr, sr = pltpu.roll(m, clon - 1, 1), pltpu.roll(s, clon - 1, 1)
        return jnp.where(last_lane, sr, mr), jnp.where(last_lane, mr, sr)

    def lon_down(m, s):
        mr, sr = pltpu.roll(m, 1, 1), pltpu.roll(s, 1, 1)
        return jnp.where(first_lane, sr, mr), jnp.where(first_lane, mr, sr)

    def term_parts(rnd):
        flat = terms[rnd].reshape(n_blocks, clon)
        halves = [jnp.where(lane >= middle, flat, 0.0), jnp.where(lane < middle, flat, 0.0)]
        return split3(flat), split3(jnp.concatenate(halves, axis=0))

    def load_window(rnd):
        main_parts, side_parts = term_parts(rnd)
        field[0] = dot3(hot_main[...], main_parts).reshape(PAD_WIN, cap, clon)
        field[1] = dot3(hot_side[...], side_parts).reshape(PAD_WIN, cap, clon)

    def adjoint(rate, main, side, first, last):
        a, b, e, f, keep = range(5)
        for _ in range(STEPS):
            a_main = {d: rate(a, 0, d) * main[d] for d in range(first + 2, last + 1)}
            b_main = {d: rate(b, 0, d) * main[d] for d in range(first, last - 1)}
            a_side = {d: rate(a, 1, d) * side[d] for d in range(first + 3, last)}
            b_side = {d: rate(b, 1, d) * side[d] for d in range(first + 1, last - 2)}
            new_main, new_side = {}, {}
            for d in range(first + 1, last):
                up = lon_up(rate(e, 0, d) * main[d], rate(e, 1, d) * side[d])
                down = lon_down(rate(f, 0, d) * main[d], rate(f, 1, d) * side[d])
                new_main[d] = rate(keep, 0, d) * main[d] + a_main[d + 1] + b_main[d - 1] + up[0] + down[0]
                if first + 2 <= d < last - 1:
                    new_side[d] = rate(keep, 1, d) * side[d] + a_side[d + 1] + b_side[d - 1] + up[1] + down[1]
            main, side = new_main, new_side
            first, last = first + 1, last - 1
        return main, side

    recv_wide(term_all(0))
    load_window(0)

    recv_wide(strip_all)
    for o in range(n_lon):
        from_right, from_left = strip_in[(o + 1) % n_lon], strip_in[(o - 1) % n_lon]
        for s in range(SLOT):
            for f in range(2):
                g = s * 2 + f
                right = pltpu.roll(from_right, (clon - g * HALO) % clon, 1)
                g = (SLOT + s) * 2 + f
                left = pltpu.roll(from_left, (2 * clon - HALO - g * HALO) % clon, 1)
                side_in[f, o, s] = jnp.where(lane < middle, right, left)
    recv_wide(main_all)

    def gather(ref, f, d):
        tile = None
        for b in range(cap):
            line = ref[f, owners[b], slots[b], pl.ds(lats[b] + d, 1), :]
            tile = jnp.broadcast_to(line, (cap, clon)) if tile is None else jnp.where(sub == b, line, tile)
        return tile

    for d in range(WIN):
        for side, ref in enumerate((main_in, side_in)):
            if d in (0, WIN - 1):
                if side == 0:
                    c0 = gather(ref, 0, d)
                    win_rates[1 if d == 0 else 0, d, side] = jnp.maximum(-c0 if d == 0 else c0, 0.0)
                continue
            for k, value in enumerate(split_rates(gather(ref, 0, d), gather(ref, 1, d))):
                win_rates[k, d, side] = value

    def window_model():
        a, b, e, f, keep = range(5)
        main = {d: field[0, d] for d in range(WIN)}
        side = {d: field[1, d] for d in range(1, WIN - 1)}
        main, side = adjoint(lambda k, n, d: win_rates[k, d, n], main, side, 0, WIN - 1)
        for d in list(main):
            lat_now = lat_tile + (li * clat + d - HALO)
            inside = (lat_now >= 0) & (lat_now < n_lat * clat)
            main[d] = jnp.where(inside, main[d], 0.0)
            if d in side:
                side[d] = jnp.where(inside, side[d], 0.0)
        for step in range(STEPS):
            reach = STEPS - 1 - step
            new_main, new_side = {}, {}
            for d in range(HALO - reach, HALO + reach + 1):
                down, up = lon_down(main[d], side[d]), lon_up(main[d], side[d])
                new_main[d] = (win_rates[keep, d, 0] * main[d] + win_rates[a, d, 0] * main[d - 1] + win_rates[b, d, 0] * main[d + 1]
                               + win_rates[e, d, 0] * down[0] + win_rates[f, d, 0] * up[0])
                if abs(d - HALO) < reach:
                    new_side[d] = (win_rates[keep, d, 1] * side[d] + win_rates[a, d, 1] * side[d - 1]
                                   + win_rates[b, d, 1] * side[d + 1] + win_rates[e, d, 1] * down[1] + win_rates[f, d, 1] * up[1])
            main, side = new_main, new_side
        seen = main[HALO]
        return [jnp.sum(obs_v[b] * seen[b:b + 1, :], axis=1, keepdims=True) for b in range(cap)]

    def recv_dense():
        for d in (-1, 1):
            def wait_lat(d=d):
                lat_make(d).wait_recv()
            guarded(-d, wait_lat)
        for d in (-1, 1, 0):
            def wait_lon(d=d):
                for role in range(2):
                    lon_make(role, d).wait_recv()
            guarded(-d, wait_lon)
        for t in range(tiles):
            for d in range(ring):
                lat = d - STEPS
                if lat < 0:
                    main = [lat_in[0, f, d, t] for f in range(2)]
                    slot = 0
                elif lat >= clat:
                    main = [lat_in[1, f, lat - clat, t] for f in range(2)]
                    slot = 2
                else:
                    main = [flow_levels(f, t, lat) for f in range(2)]
                    slot = 1
                at = lat % clat * width
                side = [
                    jnp.where(lane < middle, pltpu.roll(lon_in[0, slot, f, t], (clon - at) % clon, 1),
                              pltpu.roll(lon_in[1, slot, f, t], (2 * clon - width - at) % clon, 1))
                    for f in range(2)
                ]
                for n, pair in enumerate((main, side)):
                    for k, value in enumerate(split_rates(*pair)):
                        dense_rates[k, n, t, d] = value

    def dense(rnd):
        main_parts, side_parts = term_parts(rnd)
        dense_field[0] = dot3(dense_main[...], main_parts).reshape(ring, tiles, 8, clon)
        dense_field[1] = dot3(dense_side[...], side_parts).reshape(ring, tiles, 8, clon)

        @pl.loop(0, tiles)
        def _(t):
            main = {d: dense_field[0, d, t] for d in range(ring)}
            side = {d: dense_field[1, d, t] for d in range(1, ring - 1)}
            main, _ = adjoint(lambda k, n, d: dense_rates[k, n, t, d], main, side, 0, ring - 1)
            for lat in range(clat):
                parts[rnd, t, lat] = main[lat + STEPS]

    def red_lon_make(j):
        return pltpu.make_async_remote_copy(
            src_ref=red_lon.at[lo], dst_ref=red_lon.at[lo],
            send_sem=red_sems.at[0], recv_sem=red_sems.at[1],
            device_id={"lat": li, "lon": lon_at(j)}, device_id_type=MESH)

    def red_lat_make(j):
        return pltpu.make_async_remote_copy(
            src_ref=red_lat.at[li], dst_ref=red_lat.at[li],
            send_sem=red_sems.at[2], recv_sem=red_sems.at[3],
            device_id={"lat": lax.rem(li + j, n_lat), "lon": lo}, device_id_type=MESH)

    def red_all(ref, size, n):
        whole = ref.at[pl.ds(0, size)]
        return pltpu.make_async_remote_copy(
            src_ref=whole, dst_ref=whole, send_sem=red_sems.at[n], recv_sem=red_sems.at[n + 1],
            device_id={"lat": li, "lon": lon_at(1)}, device_id_type=MESH)

    def packed(cols):
        tile = jnp.zeros((clon, clon), F32)
        for b in range(cap):
            tile = jnp.where(lane == b, cols[b], tile)
        return tile

    p1 = window_model()
    spread(1, [weight_wide[b] * p1[b] for b in range(cap)])
    send_dense()
    build_dense()
    recv_wide(term_all(1))
    load_window(1)
    g1 = window_model()
    spread(2, [weight_wide[b] * g1[b] for b in range(cap)])
    p_all, g_all = packed(p1), packed(g1)
    u_all = columns * p_all
    tile = jnp.zeros((8, clon), F32)
    for n, value in enumerate((pltpu.roll(columns, clon - cap, 1) * p_all, u_all * p_all, u_all * g_all, columns * g_all * g_all)):
        tile = jnp.where(sub == n, jnp.sum(value, axis=0, keepdims=True), tile)
    red_lon[lo] = tile
    for j in range(1, n_lon):
        red_lon_make(j).start()
    recv_dense()
    dense(0)
    red_all(red_lon, n_lon - 1, 0).wait_recv()
    red_lat[li] = jnp.sum(red_lon[...], axis=0)

    @pl.loop(1, n_lat)
    def _(j):
        red_lat_make(j).start()

    dense(1)
    recv_wide(term_all(2))
    dense(2)
    red_all(red_lat, n_lat - 1, 2).wait_recv()

    sums = jnp.sum(jnp.sum(red_lat[...], axis=0), axis=1, keepdims=True)
    bb, s1, tt, s3 = (sums[n:n + 1] for n in range(4))
    scale = bb + s1
    alpha1, left1 = bb / scale, s1 / scale
    rr = left1 * (left1 * bb - alpha1 * s1) - alpha1 * (left1 * s1 - alpha1 * tt)
    sr1 = left1 * s1 - alpha1 * tt
    srr = left1 * sr1 - alpha1 * (left1 * tt - alpha1 * s3)
    beta = rr / bb
    curve = rr + beta * beta * bb + (srr + 2.0 * beta * sr1 + beta * beta * s1)
    alpha2 = rr / curve
    mix = left1 + beta
    inc_b, inc_t = alpha1 + alpha2 * mix, -alpha2 * alpha1
    res_b, res_t, res_2 = left1 - alpha2 * mix, -alpha1 - alpha2 * (mix - alpha1), alpha2 * alpha1
    for t in range(tiles):
        for lat in range(clat):
            b0, t1, t2 = (parts[rnd, t, lat] for rnd in range(3))
            rows = pl.ds(t * 8 * clat + lat, 8, stride=clat)
            inc_out[rows, :] = inc_b * b0 + inc_t * t1
            res_out[rows, :] = res_b * b0 + res_t * t1 + res_2 * t2

    for whole in (code_all, ask_all, main_all, strip_all, term_all(0), term_all(1), term_all(2)):
        done_wide(whole)
    for d in (-1, 1):
        def sent_lat(d=d):
            lat_make(d).wait_send()
        guarded(d, sent_lat)
    for d in (-1, 1, 0):
        def sent_lon(d=d):
            for role in range(2):
                lon_make(role, d).wait_send()
        guarded(d, sent_lon)
    red_all(red_lon, n_lon - 1, 0).wait_send()
    red_all(red_lat, n_lat - 1, 2).wait_send()


def store_kernel(inc, res, inc_out, res_out, sems):
    pairs = ((inc, inc_out), (res, res_out))
    copies = [pltpu.make_async_copy(src, dst, sems.at[n]) for n, (src, dst) in enumerate(pairs)]
    for copy in copies:
        copy.start()
    for copy in copies:
        copy.wait()


def shards(n_lat, n_lon, courant, obs_matrix, obs_weight, innovation, block_owner, block_row, block_count):
    _, levels, clat, clon = courant.shape
    cap = block_row.shape[1]
    tiles = levels // 8
    ring = clat + 2 * STEPS
    rows = clat + 2 * HALO
    unit = clon // cap
    src_pad = -(-3 * n_lon // unit) * unit
    n_blocks = src_pad * cap
    anywhere = pl.BlockSpec(memory_space=pl.ANY)
    dma = pltpu.SemaphoreType.DMA

    def f32(*shape):
        return pltpu.VMEM(shape, F32)

    def bf16(*shape):
        return pltpu.VMEM(shape, BF16)

    def i32(*shape):
        return pltpu.SMEM(shape, jnp.int32)

    flat = (levels * clat, clon)
    fields = pl.pallas_call(
        functools.partial(kernel, n_lat, n_lon),
        out_shape=(f32(*flat), f32(*flat)),
        in_specs=[anywhere] * 8,
        out_specs=(pl.BlockSpec(memory_space=pltpu.VMEM),) * 2,
        scratch_shapes=[
            f32(2, levels, clat, clon),
            f32(2 * levels * clat, clon),
            f32(cap, clon, clon),
            f32(3, src_pad, cap, clon),
            f32(3 * n_lon, 1, clon),
            f32(3, 1, clon),
            bf16(PAD_WIN * cap, n_blocks),
            bf16(PAD_WIN * cap, 2 * n_blocks),
            bf16(ring * levels, n_blocks),
            bf16(ring * levels, 2 * n_blocks),
            f32(2, PAD_WIN, cap, clon),
            f32(2, ring, tiles, 8, clon),
            f32(n_lon, 2, SLOT, clat, clon),
            f32(2, n_lon, 2, SLOT, HALO, clon),
            f32(n_lon, clat, clon),
            f32(2, n_lon, HALO, clon),
            f32(2, n_lon, SLOT, rows, clon),
            f32(n_lon, rows, clon),
            f32(2, n_lon, SLOT, rows, clon),
            f32(5, WIN, 2, cap, clon),
            f32(2, 2, STEPS, tiles, 8, clon),
            f32(2, 2, STEPS, tiles, 8, clon),
            f32(2, 2, tiles, 8, clon),
            f32(2, 3, 2, tiles, 8, clon),
            f32(5, 2, tiles, ring, 8, clon),
            f32(cap, clon, clon),
            f32(3, tiles, clat, 8, clon),
            f32(n_lon, 8, clon),
            f32(n_lat, 8, clon),
            i32(1, n_lon * SLOT),
            i32(3 * n_lon, 1, n_lon * SLOT),
            dma, dma, dma,
            dma((7, 3)), dma((7, 3)),
            dma((2,)), dma((2,)),
            dma((2, 3)), dma((2, 3)),
            dma((4,)),
            f32(1, cap, clon), f32(1, cap, clon),
            i32(1, cap), i32(1, cap), i32(1, 1),
            dma((5,)),
        ],
        compiler_params=pltpu.CompilerParams(collective_id=0, has_side_effects=True),
    )(courant, courant.reshape(2 * levels * clat, clon), obs_matrix, obs_weight, innovation, block_owner[:, :, 0], block_row, block_count)
    out = jax.ShapeDtypeStruct(flat, F32)
    stored = pl.pallas_call(
        store_kernel,
        out_shape=(out, out),
        in_specs=[anywhere] * 2,
        out_specs=(anywhere,) * 2,
        scratch_shapes=[dma((2,))],
    )(*[pltpu.with_memory_space_constraint(field, pltpu.VMEM) for field in fields])
    return tuple(field.reshape(levels, clat, clon) for field in stored)


def solution(mesh):
    placed = (
        P(None, None, "lat", "lon"),
        P("lat", "lon", None, None),
        P("lat", "lon", None),
        P("lat", "lon", None),
        P("lat", "lon", None),
        P("lat", "lon"),
        P("lat", "lon"),
    )
    return jax.shard_map(
        functools.partial(shards, mesh.shape["lat"], mesh.shape["lon"]),
        mesh=mesh,
        in_specs=placed,
        out_specs=(P(None, "lat", "lon"), P(None, "lat", "lon")),
        check_vma=False,
    )
```

time: 36.8 us -> 31.7 us (0.86)
  Pallas kernels: 33.1 us -> 30.2 us
  local copies, waits for them, and re-layouts: 2.26 us -> 0 us
    pallas_call x1 -> x2, Pallas kernels: 33.1 us -> 30.2 us  [the longest x1 29.5 us: shards(): pl.pallas_call(functools.partial(kernel, n_lat, n_lon), out_shape=(f32(*f...]
    unnamed x4 -> x0, local copies, waits for them, and re-layouts: 2.26 us -> none
where the time goes in v2:
time: 31.7 us; the launch traced here: 31.5 us
  Pallas kernels  30.2 us (95%)
  between operations  1.29 us (4%)
    pallas_call x1, Pallas kernels, shards(): pl.pallas_call(functools.partial(kernel, n_lat, n_lon), out_shape=(f32(*f...  29.5 us
    pallas_call x1, Pallas kernels, shards(): pl.pallas_call(store_kernel, out_shape=(out, out), in_specs=[anywhere] *...  0.72 us

profile of v2, /device:TPU:0, one launch (start us, length us, event | category | flops | bytes accessed | tf_op | source)
XLA Modules:
  0.0 31.5 jit_solution(954317633570310252)
XLA Ops:
  1.3 29.5 %shard_map.86 = (f32[256,128]{1,0:T(8,128)S(1)}, f32[256,128]{1,0:T(8,128)S(1)}) custom-call(f32[2,16,16,128]{3,2,1,0:T(8,128)} %courant.1, f32[512,128]{1,0:T(8,128)} %bitcast.4, f32[1,8,128,128]{3,2,1,0:T(8,128)} %obs.1, f32[1,8,128]{2,1,0:T(8,128)} %weight_in.1, f32[1,8,128]{2,1,0:T(8,128)} %innov_in.1, s32[1,8]{1,0:T(1,128)} %bitcast.5, s32[1,8]{1,0:T(1,128)} %row_in.1, ...), custom_call_target="tpu_custom_call" | custom-call | tf_op jit(solution)/shard_map/pallas_call | solution.py:671
  30.8 0.7 %shard_map.87 = (f32[256,128]{1,0:T(8,128)}, f32[256,128]{1,0:T(8,128)}) custom-call(f32[256,128]{1,0:T(8,128)S(1)} %get-tuple-element.6.inc, f32[256,128]{1,0:T(8,128)S(1)} %get-tuple-element.7.res), custom_call_target="tpu_custom_call" | custom-call | tf_op jit(solution)/shard_map/pallas_call | solution.py:720

commit v3 on v2

--- a/solution.py
+++ b/solution.py
@@ -10,6 +10,7 @@
 STEPS = 4
 HALO = 2 * STEPS
 SLOT = 2
+DIRECT = 64
 WIN = 2 * HALO + 1
 PAD_WIN = WIN + 1
 MESH = pl.DeviceIdType.MESH
@@ -17,15 +18,12 @@
 BF16 = jnp.bfloat16
 
 
-def split3(x):
+def split2(x):
     hi = x.astype(BF16)
-    rest = x - hi.astype(F32)
-    mid = rest.astype(BF16)
-    low = (rest - mid.astype(F32)).astype(BF16)
-    return hi, mid, low
-
-
-def dot3(onehot, parts):
+    return hi, (x - hi.astype(F32)).astype(BF16)
+
+
+def dot2(onehot, parts):
     total = None
     for part in parts:
         term = jnp.dot(onehot, part, preferred_element_type=F32)
@@ -45,9 +43,9 @@
     inc_out, res_out,
     flow, flow_flat, obs_v, terms, codes, code_out, hot_main, hot_side, dense_main, dense_side, field, dense_field,
     main_out, main_edge, strip_out, strip_edge, main_in, strip_in, side_in,
-    win_rates, lat_out, lat_in, lon_out, lon_in, dense_rates, weight_wide, parts, red_lon, red_lat,
+    win_rates, lat_out, lat_in, lon_out, lon_in, lon_edge_out, lon_edge_in, dense_rates, weight_wide, parts, red_lon, red_far,
     ask_out, ask_in,
-    obs_sem, flow_sem, flat_sem, wide_send, wide_recv, lat_send, lat_recv, lon_send, lon_recv, red_sems,
+    obs_sem, flow_sem, flat_sem, wide_send, wide_recv, ask_recv, lat_send, lat_recv, lon_send, lon_recv, red_sems,
     weight, innov, owner, row, count, input_sems,
 ):
     li = lax.axis_index("lat")
@@ -61,6 +59,8 @@
     span = 4 * clat
     ring = clat + 2 * STEPS
     width = clon // clat
+    n_all = n_lat * n_lon
+    direct = n_all <= DIRECT
 
     small = [
         pltpu.make_async_copy(src, dst, input_sems.at[n])
@@ -93,17 +93,22 @@
     def greet(lat, lon):
         pl.semaphore_signal(barrier, inc=1, device_id={"lat": lat, "lon": lon}, device_id_type=MESH)
 
-    @pl.loop(1, n_lat)
-    def _(j):
-        greet(lax.rem(li + j, n_lat), lo)
-
-    for d in (-1, 1):
-        def hello(d=d):
-            for j in range(1, n_lon):
-                greet(li + d, lon_at(j))
-        guarded(d, hello)
-    for j in range(1, n_lon):
-        greet(li, lon_at(j))
+    if direct:
+        for j in range(1, n_all):
+            other = lax.rem(li * n_lon + lo + j, n_all)
+            greet(lax.div(other, n_lon), lax.rem(other, n_lon))
+    else:
+        @pl.loop(1, n_lat)
+        def _(j):
+            greet(lax.rem(li + j, n_lat), lo)
+
+        for d in (-1, 1):
+            def hello(d=d):
+                for j in range(1, n_lon):
+                    greet(li + d, lon_at(j))
+            guarded(d, hello)
+        for j in range(1, n_lon):
+            greet(li, lon_at(j))
 
     for copy in small:
         copy.wait()
@@ -146,8 +151,11 @@
     for d in (-1, 0, 1):
         code_out[d + 1] = (code_line - clat * d).astype(F32)
 
-    sides = (li > 0).astype(jnp.int32) + (li < n_lat - 1).astype(jnp.int32)
-    pl.semaphore_wait(barrier, (n_lon - 1) + (n_lat - 1) + sides * (n_lon - 1))
+    if direct:
+        pl.semaphore_wait(barrier, n_all - 1)
+    else:
+        sides = (li > 0).astype(jnp.int32) + (li < n_lat - 1).astype(jnp.int32)
+        pl.semaphore_wait(barrier, (n_lon - 1) + (n_lat - 1) + sides * (n_lon - 1))
 
     def wide(kind, d, j, src, dst):
         return pltpu.make_async_remote_copy(
@@ -191,8 +199,11 @@
         ref = codes.at[pl.ds((1 - d) * n_lon, several(d))]
         return 0, ref, ref
 
-    def ask_make(d, j):
-        return wide(1, d, j, ask_out, ask_in.at[slot_of(d, j, True)])
+    def ask_make(d, j, out=True):
+        return pltpu.make_async_remote_copy(
+            src_ref=ask_out, dst_ref=ask_in.at[slot_of(d, j, out)],
+            send_sem=wide_send.at[1, d + 1], recv_sem=ask_recv.at[d + 1, j],
+            device_id={"lat": li + d, "lon": lon_at(j)}, device_id_type=MESH)
 
     def ask_all(d):
         ref = ask_in.at[pl.ds((1 - d) * n_lon, several(d))]
@@ -232,15 +243,19 @@
             return 4 + rnd, ref, ref
         return whole
 
-    def lat_make(d):
+    def lat_make(f, d):
         return pltpu.make_async_remote_copy(
-            src_ref=lat_out.at[(d + 1) // 2], dst_ref=lat_in.at[(1 - d) // 2],
-            send_sem=lat_send.at[(d + 1) // 2], recv_sem=lat_recv.at[(d + 1) // 2],
+            src_ref=lat_out.at[f, (d + 1) // 2], dst_ref=lat_in.at[f, (1 - d) // 2],
+            send_sem=lat_send.at[f, (d + 1) // 2], recv_sem=lat_recv.at[f, (d + 1) // 2],
             device_id={"lat": li + d, "lon": lo}, device_id_type=MESH)
 
     def lon_make(role, d):
+        if d == 0:
+            src, dst = lon_out.at[role], lon_in.at[role]
+        else:
+            src, dst = lon_edge_out.at[role, (d + 1) // 2], lon_edge_in.at[role, (1 - d) // 2]
         return pltpu.make_async_remote_copy(
-            src_ref=lon_out.at[role], dst_ref=lon_in.at[role, 1 - d],
+            src_ref=src, dst_ref=dst,
             send_sem=lon_send.at[role, d + 1], recv_sem=lon_recv.at[role, d + 1],
             device_id={"lat": li + d, "lon": lon_at(-1 if role == 0 else 1)}, device_id_type=MESH)
 
@@ -272,6 +287,40 @@
 
     obs_copy.wait()
     spread(0, wy_col)
+
+    flat_copy.wait()
+    for f in range(2):
+        for t in range(tiles):
+            for k in range(STEPS):
+                lat_out[f, 0, k, t] = flow_levels(f, t, k)
+                lat_out[f, 1, k, t] = flow_levels(f, t, clat - STEPS + k)
+    lane_lat = lane // width
+    bunch = STEPS * width
+    lane_bunch = lane // bunch
+    for role in range(2):
+        edges = [jnp.zeros((8, clon), F32)] * 2
+        for f in range(2):
+            for t in range(tiles):
+                tile = jnp.zeros((8, clon), F32)
+                for n in range(clat):
+                    at = (n * width + role * width) % clon
+                    tile = jnp.where(lane_lat == n, pltpu.roll(flow_levels(f, t, n), at, 1), tile)
+                lon_out[role, f, t] = tile
+                i = f * tiles + t
+                for k, at in enumerate((i * bunch, (clon + i * bunch - (clat - STEPS) * width) % clon)):
+                    edges[k] = jnp.where(lane_bunch == i, pltpu.roll(tile, at, 1), edges[k])
+        for k in range(2):
+            lon_edge_out[role, k] = edges[k]
+
+    def send_dense(f):
+        for d in (-1, 1):
+            def send(d=d):
+                lat_make(f, d).start()
+                lon_make(f, d).start()
+            guarded(d, send)
+        lon_make(f, 0).start()
+
+    send_dense(1)
 
     group = lane // HALO
 
@@ -317,42 +366,18 @@
             main_make(d, j).start()
             strip_make(d, j).start()
 
-    recv_wide(ask_all)
-    for d in (-1, 1, 0):
-        def respond(d=d):
-            for j in range(n_lon):
-                if (d, j) != (0, 0):
-                    answer(d, j)
-        guarded(d, respond)
+    def respond(d, j):
+        def run():
+            ask_make(-d, (n_lon - j) % n_lon, False).wait_recv()
+            answer(d, j)
+        guarded(d, run)
+
     answer(0, 0)
-
-    def send_dense():
-        flat_copy.wait()
-        for f in range(2):
-            for t in range(tiles):
-                for k in range(STEPS):
-                    lat_out[0, f, k, t] = flow_levels(f, t, k)
-                    lat_out[1, f, k, t] = flow_levels(f, t, clat - STEPS + k)
-        for d in (-1, 1):
-            def send_lat(d=d):
-                lat_make(d).start()
-            guarded(d, send_lat)
-        lane_lat = lane // width
-        for f in range(2):
-            for t in range(tiles):
-                right = jnp.zeros((8, clon), F32)
-                left = jnp.zeros((8, clon), F32)
-                for n in range(clat):
-                    rows = flow_levels(f, t, n)
-                    right = jnp.where(lane_lat == n, pltpu.roll(rows, n * width, 1), right)
-                    left = jnp.where(lane_lat == n, pltpu.roll(rows, (n * width + width) % clon, 1), left)
-                lon_out[0, f, t] = right
-                lon_out[1, f, t] = left
-        for d in (-1, 1, 0):
-            def send_lon(d=d):
-                for role in range(2):
-                    lon_make(role, d).start()
-            guarded(d, send_lon)
+    near = [j for j in range(1, n_lon) if 2 * j != n_lon]
+    far = [j for j in range(1, n_lon) if 2 * j == n_lon]
+    for d, js in ((0, near), (1, [0]), (-1, [0]), (0, far), (1, near), (-1, near), (1, far), (-1, far)):
+        for j in js:
+            respond(d, j)
 
     pad = terms.shape[1] - n_src
     if pad:
@@ -368,8 +393,8 @@
             lat0 = 0 if d == -1 else HALO + clat
             main_in[:, :, :, lat0:lat0 + HALO, :] = jnp.zeros((2, n_lon, SLOT, HALO, clon), F32)
             strip_in[:, lat0:lat0 + HALO, :] = jnp.zeros((n_lon, HALO, clon), F32)
-            lat_in[(d + 1) // 2] = jnp.zeros((2, STEPS, tiles, 8, clon), F32)
-            lon_in[:, d + 1] = jnp.zeros((2, 2, tiles, 8, clon), F32)
+            lat_in[:, (d + 1) // 2] = jnp.zeros((2, STEPS, tiles, 8, clon), F32)
+            lon_edge_in[:, (d + 1) // 2] = jnp.zeros((2, 8, clon), F32)
 
     recv_wide(code_all)
     code_parts = []
@@ -421,12 +446,12 @@
     def term_parts(rnd):
         flat = terms[rnd].reshape(n_blocks, clon)
         halves = [jnp.where(lane >= middle, flat, 0.0), jnp.where(lane < middle, flat, 0.0)]
-        return split3(flat), split3(jnp.concatenate(halves, axis=0))
+        return split2(flat), split2(jnp.concatenate(halves, axis=0))
 
     def load_window(rnd):
         main_parts, side_parts = term_parts(rnd)
-        field[0] = dot3(hot_main[...], main_parts).reshape(PAD_WIN, cap, clon)
-        field[1] = dot3(hot_side[...], side_parts).reshape(PAD_WIN, cap, clon)
+        field[0] = dot2(hot_main[...], main_parts).reshape(PAD_WIN, cap, clon)
+        field[1] = dot2(hot_side[...], side_parts).reshape(PAD_WIN, cap, clon)
 
     def adjoint(rate, main, side, first, last):
         a, b, e, f, keep = range(5)
@@ -460,6 +485,7 @@
                 left = pltpu.roll(from_left, (2 * clon - HALO - g * HALO) % clon, 1)
                 side_in[f, o, s] = jnp.where(lane < middle, right, left)
     recv_wide(main_all)
+    send_dense(0)
 
     def gather(ref, f, d):
         tile = None
@@ -503,42 +529,43 @@
         seen = main[HALO]
         return [jnp.sum(obs_v[b] * seen[b:b + 1, :], axis=1, keepdims=True) for b in range(cap)]
 
+    def each_dense(run):
+        for f in range(2):
+            for d in (-1, 1, 0):
+                def go(f=f, d=d):
+                    if d:
+                        run(lat_make(f, d))
+                    run(lon_make(f, d))
+                yield d, go
+
     def recv_dense():
-        for d in (-1, 1):
-            def wait_lat(d=d):
-                lat_make(d).wait_recv()
-            guarded(-d, wait_lat)
-        for d in (-1, 1, 0):
-            def wait_lon(d=d):
-                for role in range(2):
-                    lon_make(role, d).wait_recv()
-            guarded(-d, wait_lon)
+        for d, go in each_dense(lambda copy: copy.wait_recv()):
+            guarded(-d, go)
         for t in range(tiles):
             for d in range(ring):
                 lat = d - STEPS
                 if lat < 0:
-                    main = [lat_in[0, f, d, t] for f in range(2)]
-                    slot = 0
+                    main, edge, at = [lat_in[f, 0, d, t] for f in range(2)], 0, d
                 elif lat >= clat:
-                    main = [lat_in[1, f, lat - clat, t] for f in range(2)]
-                    slot = 2
+                    main, edge, at = [lat_in[f, 1, lat - clat, t] for f in range(2)], 1, lat - clat
                 else:
-                    main = [flow_levels(f, t, lat) for f in range(2)]
-                    slot = 1
-                at = lat % clat * width
-                side = [
-                    jnp.where(lane < middle, pltpu.roll(lon_in[0, slot, f, t], (clon - at) % clon, 1),
-                              pltpu.roll(lon_in[1, slot, f, t], (2 * clon - width - at) % clon, 1))
-                    for f in range(2)
-                ]
+                    main, edge, at = [flow_levels(f, t, lat) for f in range(2)], None, lat
+                side = []
+                for f in range(2):
+                    if edge is None:
+                        first, pair = at * width, [lon_in[role, f, t] for role in range(2)]
+                    else:
+                        first, pair = (f * tiles + t) * bunch + at * width, [lon_edge_in[role, edge] for role in range(2)]
+                    side.append(jnp.where(lane < middle, pltpu.roll(pair[0], (clon - first) % clon, 1),
+                                          pltpu.roll(pair[1], (2 * clon - width - first) % clon, 1)))
                 for n, pair in enumerate((main, side)):
                     for k, value in enumerate(split_rates(*pair)):
                         dense_rates[k, n, t, d] = value
 
     def dense(rnd):
         main_parts, side_parts = term_parts(rnd)
-        dense_field[0] = dot3(dense_main[...], main_parts).reshape(ring, tiles, 8, clon)
-        dense_field[1] = dot3(dense_side[...], side_parts).reshape(ring, tiles, 8, clon)
+        dense_field[0] = dot2(dense_main[...], main_parts).reshape(ring, tiles, 8, clon)
+        dense_field[1] = dot2(dense_side[...], side_parts).reshape(ring, tiles, 8, clon)
 
         @pl.loop(0, tiles)
         def _(t):
@@ -548,23 +575,39 @@
             for lat in range(clat):
                 parts[rnd, t, lat] = main[lat + STEPS]
 
-    def red_lon_make(j):
+    def red_make(n, ref, own, lat, lon):
         return pltpu.make_async_remote_copy(
-            src_ref=red_lon.at[lo], dst_ref=red_lon.at[lo],
-            send_sem=red_sems.at[0], recv_sem=red_sems.at[1],
-            device_id={"lat": li, "lon": lon_at(j)}, device_id_type=MESH)
-
-    def red_lat_make(j):
-        return pltpu.make_async_remote_copy(
-            src_ref=red_lat.at[li], dst_ref=red_lat.at[li],
-            send_sem=red_sems.at[2], recv_sem=red_sems.at[3],
-            device_id={"lat": lax.rem(li + j, n_lat), "lon": lo}, device_id_type=MESH)
-
-    def red_all(ref, size, n):
+            src_ref=ref.at[own], dst_ref=ref.at[own], send_sem=red_sems.at[n], recv_sem=red_sems.at[n + 1],
+            device_id={"lat": lat, "lon": lon}, device_id_type=MESH)
+
+    def red_all(n, ref, size):
         whole = ref.at[pl.ds(0, size)]
         return pltpu.make_async_remote_copy(
             src_ref=whole, dst_ref=whole, send_sem=red_sems.at[n], recv_sem=red_sems.at[n + 1],
             device_id={"lat": li, "lon": lon_at(1)}, device_id_type=MESH)
+
+    def reduce_start(line):
+        if direct:
+            me = li * n_lon + lo
+            red_far[me] = line
+            for j in range(1, n_all):
+                other = lax.rem(me + j, n_all)
+                red_make(2, red_far, me, lax.div(other, n_lon), lax.rem(other, n_lon)).start()
+        else:
+            red_lon[lo] = line
+            for j in range(1, n_lon):
+                red_make(0, red_lon, lo, li, lon_at(j)).start()
+
+    def reduce_turn():
+        if not direct:
+            red_all(0, red_lon, n_lon - 1).wait_recv()
+            red_far[li] = jnp.sum(red_lon[...], axis=0)
+
+            @pl.loop(1, n_lat)
+            def _(j):
+                red_make(2, red_far, li, lax.rem(li + j, n_lat), lo).start()
+
+    far_size = n_all if direct else n_lat
 
     def packed(cols):
         tile = jnp.zeros((clon, clon), F32)
@@ -574,7 +617,6 @@
 
     p1 = window_model()
     spread(1, [weight_wide[b] * p1[b] for b in range(cap)])
-    send_dense()
     build_dense()
     recv_wide(term_all(1))
     load_window(1)
@@ -582,28 +624,21 @@
     spread(2, [weight_wide[b] * g1[b] for b in range(cap)])
     p_all, g_all = packed(p1), packed(g1)
     u_all = columns * p_all
-    tile = jnp.zeros((8, clon), F32)
+    line = jnp.zeros((1, clon), F32)
     for n, value in enumerate((pltpu.roll(columns, clon - cap, 1) * p_all, u_all * p_all, u_all * g_all, columns * g_all * g_all)):
-        tile = jnp.where(sub == n, jnp.sum(value, axis=0, keepdims=True), tile)
-    red_lon[lo] = tile
-    for j in range(1, n_lon):
-        red_lon_make(j).start()
+        line = line + pltpu.roll(jnp.sum(value, axis=0, keepdims=True), n * cap, 1)
+    reduce_start(line)
     recv_dense()
     dense(0)
-    red_all(red_lon, n_lon - 1, 0).wait_recv()
-    red_lat[li] = jnp.sum(red_lon[...], axis=0)
-
-    @pl.loop(1, n_lat)
-    def _(j):
-        red_lat_make(j).start()
-
+    reduce_turn()
     dense(1)
     recv_wide(term_all(2))
     dense(2)
-    red_all(red_lat, n_lat - 1, 2).wait_recv()
-
-    sums = jnp.sum(jnp.sum(red_lat[...], axis=0), axis=1, keepdims=True)
-    bb, s1, tt, s3 = (sums[n:n + 1] for n in range(4))
+    red_all(2, red_far, far_size - 1).wait_recv()
+
+    line = jnp.sum(red_far[...], axis=0)
+    sums = [jnp.sum(jnp.where(lane // cap == n, line, 0.0), axis=1, keepdims=True) for n in range(4)]
+    bb, s1, tt, s3 = sums
     scale = bb + s1
     alpha1, left1 = bb / scale, s1 / scale
     rr = left1 * (left1 * bb - alpha1 * s1) - alpha1 * (left1 * s1 - alpha1 * tt)
@@ -624,17 +659,11 @@
 
     for whole in (code_all, ask_all, main_all, strip_all, term_all(0), term_all(1), term_all(2)):
         done_wide(whole)
-    for d in (-1, 1):
-        def sent_lat(d=d):
-            lat_make(d).wait_send()
-        guarded(d, sent_lat)
-    for d in (-1, 1, 0):
-        def sent_lon(d=d):
-            for role in range(2):
-                lon_make(role, d).wait_send()
-        guarded(d, sent_lon)
-    red_all(red_lon, n_lon - 1, 0).wait_send()
-    red_all(red_lat, n_lat - 1, 2).wait_send()
+    for d, go in each_dense(lambda copy: copy.wait_send()):
+        guarded(d, go)
+    if not direct:
+        red_all(0, red_lon, n_lon - 1).wait_send()
+    red_all(2, red_far, far_size - 1).wait_send()
 
 
 def store_kernel(inc, res, inc_out, res_out, sems):
@@ -697,17 +726,20 @@
             f32(2, 2, STEPS, tiles, 8, clon),
             f32(2, 2, STEPS, tiles, 8, clon),
             f32(2, 2, tiles, 8, clon),
-            f32(2, 3, 2, tiles, 8, clon),
+            f32(2, 2, tiles, 8, clon),
+            f32(2, 2, 8, clon),
+            f32(2, 2, 8, clon),
             f32(5, 2, tiles, ring, 8, clon),
             f32(cap, clon, clon),
             f32(3, tiles, clat, 8, clon),
-            f32(n_lon, 8, clon),
-            f32(n_lat, 8, clon),
+            f32(n_lon, 1, clon),
+            f32(n_lat * n_lon if n_lat * n_lon <= DIRECT else n_lat, 1, clon),
             i32(1, n_lon * SLOT),
             i32(3 * n_lon, 1, n_lon * SLOT),
             dma, dma, dma,
             dma((7, 3)), dma((7, 3)),
-            dma((2,)), dma((2,)),
+            dma((3, n_lon)),
+            dma((2, 2)), dma((2, 2)),
             dma((2, 3)), dma((2, 3)),
             dma((4,)),
             f32(1, cap, clon), f32(1, cap, clon),

time: 31.7 us -> 28.8 us (0.909)
  Pallas kernels: 30.2 us -> 27.4 us
    pallas_call x1, Pallas kernels: 29.5 us -> 26.7 us  [shards(): pl.pallas_call(functools.partial(kernel, n_lat, n_lon), out_shape=(f32(*f...]
where the time goes in v3:
time: 28.8 us; the launch traced here: 28.7 us
  Pallas kernels  27.4 us (95%)
  between operations  1.29 us (4%)
    pallas_call x1, Pallas kernels, shards(): pl.pallas_call(functools.partial(kernel, n_lat, n_lon), out_shape=(f32(*f...  26.7 us
    pallas_call x1, Pallas kernels, shards(): pl.pallas_call(store_kernel, out_shape=(out, out), in_specs=[anywhere] *...  0.72 us

profile of v3, /device:TPU:0, one launch (start us, length us, event | category | flops | bytes accessed | tf_op | source)
XLA Modules:
  0.0 28.7 jit_solution(2194835120923391196)
XLA Ops:
  1.3 26.7 %shard_map.86 = (f32[256,128]{1,0:T(8,128)S(1)}, f32[256,128]{1,0:T(8,128)S(1)}) custom-call(f32[2,16,16,128]{3,2,1,0:T(8,128)} %courant.1, f32[512,128]{1,0:T(8,128)} %bitcast.4, f32[1,8,128,128]{3,2,1,0:T(8,128)} %obs.1, f32[1,8,128]{2,1,0:T(8,128)} %weight_in.1, f32[1,8,128]{2,1,0:T(8,128)} %innov_in.1, s32[1,8]{1,0:T(1,128)} %bitcast.5, s32[1,8]{1,0:T(1,128)} %row_in.1, ...), custom_call_target="tpu_custom_call" | custom-call | tf_op jit(solution)/shard_map/pallas_call | solution.py:700
  28.0 0.7 %shard_map.87 = (f32[256,128]{1,0:T(8,128)}, f32[256,128]{1,0:T(8,128)}) custom-call(f32[256,128]{1,0:T(8,128)S(1)} %get-tuple-element.6.inc, f32[256,128]{1,0:T(8,128)S(1)} %get-tuple-element.7.res), custom_call_target="tpu_custom_call" | custom-call | tf_op jit(solution)/shard_map/pallas_call | solution.py:752

commit v4 on v3

--- a/solution.py
+++ b/solution.py
@@ -42,10 +42,10 @@
     courant, courant_flat, obs, weight_in, innov_in, owner_in, row_in, count_in,
     inc_out, res_out,
     flow, flow_flat, obs_v, terms, codes, code_out, hot_main, hot_side, dense_main, dense_side, field, dense_field,
-    main_out, main_edge, strip_out, strip_edge, main_in, strip_in, side_in,
+    main_out, main_edge, strip_out, strip_edge, main_in, strip_in, strip_edge_in, side_in,
     win_rates, lat_out, lat_in, lon_out, lon_in, lon_edge_out, lon_edge_in, dense_rates, weight_wide, parts, red_lon, red_far,
-    ask_out, ask_in,
-    obs_sem, flow_sem, flat_sem, wide_send, wide_recv, ask_recv, lat_send, lat_recv, lon_send, lon_recv, red_sems,
+    proxy, ask_out, ask_in,
+    obs_sem, flow_sem, flat_sem, wide_send, wide_recv, ask_send, ask_recv, red_sems,
     weight, innov, owner, row, count, input_sems,
 ):
     li = lax.axis_index("lat")
@@ -159,16 +159,29 @@
 
     def wide(kind, d, j, src, dst):
         return pltpu.make_async_remote_copy(
-            src_ref=src, dst_ref=dst,
-            send_sem=wide_send.at[kind, d + 1], recv_sem=wide_recv.at[kind, d + 1],
+            src_ref=src, dst_ref=dst, send_sem=wide_send.at[d + 1], recv_sem=wide_recv.at[kind],
             device_id={"lat": li + d, "lon": lon_at(j)}, device_id_type=MESH,
         )
 
+    def rows_of(sem, ref, rows):
+        whole = ref.at[pl.ds(0, rows)]
+        return pltpu.make_async_remote_copy(
+            src_ref=whole, dst_ref=whole, send_sem=sem, recv_sem=sem,
+            device_id={"lat": li, "lon": lon_at(1)}, device_id_type=MESH)
+
+    def with_sides(run):
+        both = exists(-1) & exists(1)
+        pl.when(both)(lambda: run(2))
+        pl.when(jnp.logical_not(both))(lambda: run(1))
+
+    def recv_rows(kind, own, side):
+        with_sides(lambda sides: rows_of(wide_recv.at[kind], proxy, own + sides * side).wait_recv())
+
+    def recv_wide(kind, rows):
+        recv_rows(kind, (n_lon - 1) * rows, n_lon * rows)
+
     def slot_of(d, j, out):
         return (1 - d) * n_lon + (lo if out else lon_at(-j))
-
-    def several(d):
-        return n_lon - 1 if d == 0 else n_lon
 
     def start_wide(make):
         for d in (-1, 1, 0):
@@ -178,36 +191,14 @@
                         make(d, j).start()
             guarded(d, run)
 
-    def recv_wide(whole):
-        for d in (-1, 1, 0):
-            def run(d=d):
-                kind, _, into = whole(d)
-                wide(kind, d, 1, into, into).wait_recv()
-            guarded(-d, run)
-
-    def done_wide(whole):
-        for d in (-1, 1, 0):
-            def run(d=d):
-                kind, out, _ = whole(d)
-                wide(kind, d, 1, out, out).wait_send()
-            guarded(d, run)
-
     def code_make(d, j):
         return wide(0, d, j, code_out.at[d + 1], codes.at[slot_of(d, j, True)])
-
-    def code_all(d):
-        ref = codes.at[pl.ds((1 - d) * n_lon, several(d))]
-        return 0, ref, ref
 
     def ask_make(d, j, out=True):
         return pltpu.make_async_remote_copy(
             src_ref=ask_out, dst_ref=ask_in.at[slot_of(d, j, out)],
-            send_sem=wide_send.at[1, d + 1], recv_sem=ask_recv.at[d + 1, j],
+            send_sem=ask_send, recv_sem=ask_recv.at[d + 1, j],
             device_id={"lat": li + d, "lon": lon_at(j)}, device_id_type=MESH)
-
-    def ask_all(d):
-        ref = ask_in.at[pl.ds((1 - d) * n_lon, several(d))]
-        return 1, ref, ref
 
     def place(d):
         return (HALO, clat) if d == 0 else ((0, HALO) if d == 1 else (HALO + clat, HALO))
@@ -215,49 +206,27 @@
     def main_make(d, j):
         first, size = place(d)
         src = main_out.at[j] if d == 0 else main_edge.at[(d + 1) // 2, j]
-        return wide(2, d, j, src, main_in.at[:, lo, :, pl.ds(first, size), :])
-
-    def main_all(d):
-        first, size = place(d)
-        src = main_out.at[pl.ds(1, n_lon - 1)] if d == 0 else main_edge.at[(d + 1) // 2]
-        return 2, src, main_in.at[:, pl.ds(0, several(d)), :, pl.ds(first, size), :]
+        return wide(1, d, j, src, main_in.at[:, lo, :, pl.ds(first, size), :])
 
     def strip_make(d, j):
-        first, size = place(d)
-        src = strip_out.at[j] if d == 0 else strip_edge.at[(d + 1) // 2, j]
-        return wide(3, d, j, src, strip_in.at[lo, pl.ds(first, size), :])
-
-    def strip_all(d):
-        first, size = place(d)
-        src = strip_out.at[pl.ds(1, n_lon - 1)] if d == 0 else strip_edge.at[(d + 1) // 2]
-        return 3, src, strip_in.at[pl.ds(0, several(d)), pl.ds(first, size), :]
+        if d == 0:
+            return wide(2, d, j, strip_out.at[j], strip_in.at[lo])
+        return wide(3, d, j, strip_edge.at[(d + 1) // 2, j], strip_edge_in.at[(1 - d) // 2, lo])
 
     def term_make(rnd):
         def make(d, j):
             return wide(4 + rnd, d, j, terms.at[rnd, n_lon + lo], terms.at[rnd, slot_of(d, j, True)])
         return make
 
-    def term_all(rnd):
-        def whole(d):
-            ref = terms.at[rnd, pl.ds((1 - d) * n_lon, several(d))]
-            return 4 + rnd, ref, ref
-        return whole
-
     def lat_make(f, d):
-        return pltpu.make_async_remote_copy(
-            src_ref=lat_out.at[f, (d + 1) // 2], dst_ref=lat_in.at[f, (1 - d) // 2],
-            send_sem=lat_send.at[f, (d + 1) // 2], recv_sem=lat_recv.at[f, (d + 1) // 2],
-            device_id={"lat": li + d, "lon": lo}, device_id_type=MESH)
+        return wide(7, d, 0, lat_out.at[f, (d + 1) // 2], lat_in.at[f, (1 - d) // 2])
 
     def lon_make(role, d):
         if d == 0:
             src, dst = lon_out.at[role], lon_in.at[role]
         else:
             src, dst = lon_edge_out.at[role, (d + 1) // 2], lon_edge_in.at[role, (1 - d) // 2]
-        return pltpu.make_async_remote_copy(
-            src_ref=src, dst_ref=dst,
-            send_sem=lon_send.at[role, d + 1], recv_sem=lon_recv.at[role, d + 1],
-            device_id={"lat": li + d, "lon": lon_at(-1 if role == 0 else 1)}, device_id_type=MESH)
+        return wide(7, d, -1 if role == 0 else 1, src, dst)
 
     start_wide(ask_make)
     start_wide(code_make)
@@ -338,7 +307,7 @@
                 return ask_out[0, o * SLOT + s]
             return ask_in[slot, 0, o * SLOT + s]
 
-        tile = jnp.zeros((size, clon), F32)
+        tile = jnp.zeros((HALO, clon), F32)
         for s in range(SLOT):
             lev = asked(lo, s)
             right, left = asked(lon_at(-1), s), asked(lon_at(1), s)
@@ -350,21 +319,21 @@
                     main_out[j, f, s] = rows
                 else:
                     main_edge[(d + 1) // 2, j, f, s] = rows
-                g = s * 2 + f
-                moved = pltpu.roll(flow_rows(f, right, first, size), g * HALO, 1)
-                tile = jnp.where(group == g, moved, tile)
-                g = (SLOT + s) * 2 + f
-                moved = pltpu.roll(flow_rows(f, left, first, size), (g + 1) * HALO, 1)
-                tile = jnp.where(group == g, moved, tile)
+                for k in range(size // HALO):
+                    for g, lev_now, extra in ((s * 2 + f, right, 0), ((SLOT + s) * 2 + f, left, HALO)):
+                        at = (k * middle + g * HALO + extra) % clon
+                        moved = pltpu.roll(flow_rows(f, lev_now, first + k * HALO, HALO), at, 1)
+                        tile = jnp.where(group == k * (middle // HALO) + g, moved, tile)
         if (d, j) == (0, 0):
-            strip_in[lo, HALO:HALO + clat, :] = tile
+            strip_in[lo] = tile
+            return
+        if d == 0:
+            strip_out[j] = tile
         else:
-            if d == 0:
-                strip_out[j] = tile
-            else:
-                strip_edge[(d + 1) // 2, j] = tile
-            main_make(d, j).start()
-            strip_make(d, j).start()
+            folded = pltpu.roll(pltpu.roll(tile, HALO // 2, 0), middle, 1)
+            strip_edge[(d + 1) // 2, j] = jnp.where(lane < middle, tile, folded)[:HALO // 2]
+        main_make(d, j).start()
+        strip_make(d, j).start()
 
     def respond(d, j):
         def run():
@@ -375,7 +344,7 @@
     answer(0, 0)
     near = [j for j in range(1, n_lon) if 2 * j != n_lon]
     far = [j for j in range(1, n_lon) if 2 * j == n_lon]
-    for d, js in ((0, near), (1, [0]), (-1, [0]), (0, far), (1, near), (-1, near), (1, far), (-1, far)):
+    for d, js in ((1, [0]), (-1, [0]), (1, near), (-1, near), (0, near), (1, far), (-1, far), (0, far)):
         for j in js:
             respond(d, j)
 
@@ -392,11 +361,11 @@
                 terms[rnd, first:first + n_lon] = jnp.zeros((n_lon, cap, clon), F32)
             lat0 = 0 if d == -1 else HALO + clat
             main_in[:, :, :, lat0:lat0 + HALO, :] = jnp.zeros((2, n_lon, SLOT, HALO, clon), F32)
-            strip_in[:, lat0:lat0 + HALO, :] = jnp.zeros((n_lon, HALO, clon), F32)
+            strip_edge_in[(d + 1) // 2] = jnp.zeros((n_lon, HALO // 2, clon), F32)
             lat_in[:, (d + 1) // 2] = jnp.zeros((2, STEPS, tiles, 8, clon), F32)
             lon_edge_in[:, (d + 1) // 2] = jnp.zeros((2, 8, clon), F32)
 
-    recv_wide(code_all)
+    recv_wide(0, 1)
     code_parts = []
     for first in range(0, n_blocks, clon):
         line = jnp.full((1, clon), -4.0 * span, F32)
@@ -471,20 +440,32 @@
             first, last = first + 1, last - 1
         return main, side
 
-    recv_wide(term_all(0))
+    recv_wide(4, cap)
     load_window(0)
 
-    recv_wide(strip_all)
-    for o in range(n_lon):
-        from_right, from_left = strip_in[(o + 1) % n_lon], strip_in[(o - 1) % n_lon]
-        for s in range(SLOT):
-            for f in range(2):
-                g = s * 2 + f
-                right = pltpu.roll(from_right, (clon - g * HALO) % clon, 1)
-                g = (SLOT + s) * 2 + f
-                left = pltpu.roll(from_left, (2 * clon - HALO - g * HALO) % clon, 1)
-                side_in[f, o, s] = jnp.where(lane < middle, right, left)
-    recv_wide(main_all)
+    def unpack(sources, offset, first):
+        for o in range(n_lon):
+            from_right, from_left = sources[(o + 1) % n_lon], sources[(o - 1) % n_lon]
+            for s in range(SLOT):
+                for f in range(2):
+                    at = offset + (s * 2 + f) * HALO
+                    right = pltpu.roll(from_right, (clon - at) % clon, 1)
+                    at = offset + ((SLOT + s) * 2 + f + 1) * HALO
+                    left = pltpu.roll(from_left, (2 * clon - at) % clon, 1)
+                    side_in[f, o, s, first:first + HALO, :] = jnp.where(lane < middle, right, left)
+
+    rows_of(wide_recv.at[2], proxy, (n_lon - 1) * HALO).wait_recv()
+    own_strips = [strip_in[o] for o in range(n_lon)]
+    for k in range(clat // HALO):
+        unpack(own_strips, k * middle, (k + 1) * HALO)
+    recv_rows(3, 0, n_lon * HALO // 2)
+    for k in range(2):
+        edges = []
+        for o in range(n_lon):
+            edge = strip_edge_in[k, o]
+            edges.append(jnp.concatenate([edge, pltpu.roll(edge, middle, 1)], axis=0))
+        unpack(edges, 0, k * (HALO + clat))
+    recv_rows(1, (n_lon - 1) * 2 * SLOT * clat, n_lon * 2 * SLOT * HALO)
     send_dense(0)
 
     def gather(ref, f, d):
@@ -529,18 +510,10 @@
         seen = main[HALO]
         return [jnp.sum(obs_v[b] * seen[b:b + 1, :], axis=1, keepdims=True) for b in range(cap)]
 
-    def each_dense(run):
-        for f in range(2):
-            for d in (-1, 1, 0):
-                def go(f=f, d=d):
-                    if d:
-                        run(lat_make(f, d))
-                    run(lon_make(f, d))
-                yield d, go
+    dense_own, dense_side_rows = 4 * tiles * 8, 2 * STEPS * tiles * 8 + 2 * 8
 
     def recv_dense():
-        for d, go in each_dense(lambda copy: copy.wait_recv()):
-            guarded(-d, go)
+        recv_rows(7, dense_own, dense_side_rows)
         for t in range(tiles):
             for d in range(ring):
                 lat = d - STEPS
@@ -567,7 +540,7 @@
         dense_field[0] = dot2(dense_main[...], main_parts).reshape(ring, tiles, 8, clon)
         dense_field[1] = dot2(dense_side[...], side_parts).reshape(ring, tiles, 8, clon)
 
-        @pl.loop(0, tiles)
+        @pl.loop(0, tiles, unroll=tiles)
         def _(t):
             main = {d: dense_field[0, d, t] for d in range(ring)}
             side = {d: dense_field[1, d, t] for d in range(1, ring - 1)}
@@ -618,7 +591,7 @@
     p1 = window_model()
     spread(1, [weight_wide[b] * p1[b] for b in range(cap)])
     build_dense()
-    recv_wide(term_all(1))
+    recv_wide(5, cap)
     load_window(1)
     g1 = window_model()
     spread(2, [weight_wide[b] * g1[b] for b in range(cap)])
@@ -632,7 +605,7 @@
     dense(0)
     reduce_turn()
     dense(1)
-    recv_wide(term_all(2))
+    recv_wide(6, cap)
     dense(2)
     red_all(2, red_far, far_size - 1).wait_recv()
 
@@ -657,10 +630,14 @@
             inc_out[rows, :] = inc_b * b0 + inc_t * t1
             res_out[rows, :] = res_b * b0 + res_t * t1 + res_2 * t2
 
-    for whole in (code_all, ask_all, main_all, strip_all, term_all(0), term_all(1), term_all(2)):
-        done_wide(whole)
-    for d, go in each_dense(lambda copy: copy.wait_send()):
-        guarded(d, go)
+    for d in (-1, 1, 0):
+        def sent(d=d):
+            edge = HALO if d else clat
+            strip = HALO // 2 if d else HALO
+            rows = (n_lon if d else n_lon - 1) * (1 + 2 * SLOT * edge + strip + 3 * cap)
+            rows_of(wide_send.at[d + 1], proxy, rows + (dense_side_rows if d else dense_own)).wait_send()
+        guarded(d, sent)
+    with_sides(lambda sides: rows_of(ask_send, ask_in, n_lon - 1 + sides * n_lon).wait_send())
     if not direct:
         red_all(0, red_lon, n_lon - 1).wait_send()
     red_all(2, red_far, far_size - 1).wait_send()
@@ -717,10 +694,11 @@
             f32(2, ring, tiles, 8, clon),
             f32(n_lon, 2, SLOT, clat, clon),
             f32(2, n_lon, 2, SLOT, HALO, clon),
-            f32(n_lon, clat, clon),
-            f32(2, n_lon, HALO, clon),
+            f32(n_lon, HALO, clon),
+            f32(2, n_lon, HALO // 2, clon),
             f32(2, n_lon, SLOT, rows, clon),
-            f32(n_lon, rows, clon),
+            f32(n_lon, HALO, clon),
+            f32(2, n_lon, HALO // 2, clon),
             f32(2, n_lon, SLOT, rows, clon),
             f32(5, WIN, 2, cap, clon),
             f32(2, 2, STEPS, tiles, 8, clon),
@@ -734,13 +712,11 @@
             f32(3, tiles, clat, 8, clon),
             f32(n_lon, 1, clon),
             f32(n_lat * n_lon if n_lat * n_lon <= DIRECT else n_lat, 1, clon),
+            f32(n_lon * 256, clon),
             i32(1, n_lon * SLOT),
             i32(3 * n_lon, 1, n_lon * SLOT),
             dma, dma, dma,
-            dma((7, 3)), dma((7, 3)),
-            dma((3, n_lon)),
-            dma((2, 2)), dma((2, 2)),
-            dma((2, 3)), dma((2, 3)),
+            dma((3,)), dma((8,)), dma, dma((3, n_lon)),
             dma((4,)),
             f32(1, cap, clon), f32(1, cap, clon),
             i32(1, cap), i32(1, cap), i32(1, 1),

time: 28.8 us -> 27.9 us (0.969)
  Pallas kernels: 27.4 us -> 26.5 us
    pallas_call x1, Pallas kernels: 26.7 us -> 25.8 us  [shards(): pl.pallas_call(functools.partial(kernel, n_lat, n_lon), out_shape=(f32(*f...]
where the time goes in v4:
time: 27.9 us; the launch traced here: 27.8 us
  Pallas kernels  26.5 us (95%)
  between operations  1.29 us (5%)
    pallas_call x1, Pallas kernels, shards(): pl.pallas_call(functools.partial(kernel, n_lat, n_lon), out_shape=(f32(*f...  25.8 us
    pallas_call x1, Pallas kernels, shards(): pl.pallas_call(store_kernel, out_shape=(out, out), in_specs=[anywhere] *...  0.72 us

profile of v4, /device:TPU:0, one launch (start us, length us, event | category | flops | bytes accessed | tf_op | source)
XLA Modules:
  0.0 27.8 jit_solution(1994002517866098525)
XLA Ops:
  1.3 25.8 %shard_map.86 = (f32[256,128]{1,0:T(8,128)S(1)}, f32[256,128]{1,0:T(8,128)S(1)}) custom-call(f32[2,16,16,128]{3,2,1,0:T(8,128)} %courant.1, f32[512,128]{1,0:T(8,128)} %bitcast.4, f32[1,8,128,128]{3,2,1,0:T(8,128)} %obs.1, f32[1,8,128]{2,1,0:T(8,128)} %weight_in.1, f32[1,8,128]{2,1,0:T(8,128)} %innov_in.1, s32[1,8]{1,0:T(1,128)} %bitcast.5, s32[1,8]{1,0:T(1,128)} %row_in.1, ...), custom_call_target="tpu_custom_call" | custom-call | tf_op jit(solution)/shard_map/pallas_call | solution.py:677
  27.1 0.7 %shard_map.87 = (f32[256,128]{1,0:T(8,128)}, f32[256,128]{1,0:T(8,128)}) custom-call(f32[256,128]{1,0:T(8,128)S(1)} %get-tuple-element.6.inc, f32[256,128]{1,0:T(8,128)S(1)} %get-tuple-element.7.res), custom_call_target="tpu_custom_call" | custom-call | tf_op jit(solution)/shard_map/pallas_call | solution.py:728

commit v5 on v4

--- a/solution.py
+++ b/solution.py
@@ -45,7 +45,7 @@
     main_out, main_edge, strip_out, strip_edge, main_in, strip_in, strip_edge_in, side_in,
     win_rates, lat_out, lat_in, lon_out, lon_in, lon_edge_out, lon_edge_in, dense_rates, weight_wide, parts, red_lon, red_far,
     proxy, ask_out, ask_in,
-    obs_sem, flow_sem, flat_sem, wide_send, wide_recv, ask_send, ask_recv, red_sems,
+    obs_sem, flow_sem, flat_sem, wide_send, wide_recv, ask_send, ask_recv, red_sems, token,
     weight, innov, owner, row, count, input_sems,
 ):
     li = lax.axis_index("lat")
@@ -93,22 +93,24 @@
     def greet(lat, lon):
         pl.semaphore_signal(barrier, inc=1, device_id={"lat": lat, "lon": lon}, device_id_type=MESH)
 
-    if direct:
-        for j in range(1, n_all):
-            other = lax.rem(li * n_lon + lo + j, n_all)
-            greet(lax.div(other, n_lon), lax.rem(other, n_lon))
-    else:
-        @pl.loop(1, n_lat)
+    for d in (-1, 1):
+        def hello(d=d):
+            for j in range(n_lon):
+                greet(li + d, lon_at(j))
+        guarded(d, hello)
+    for j in range(1, n_lon):
+        greet(li, lon_at(j))
+    sides = (li > 0).astype(jnp.int32) + (li < n_lat - 1).astype(jnp.int32)
+    greeted = n_lon - 1 + sides * n_lon
+    if not direct:
+        @pl.loop(2, n_lat - 1)
         def _(j):
             greet(lax.rem(li + j, n_lat), lo)
 
-        for d in (-1, 1):
-            def hello(d=d):
-                for j in range(1, n_lon):
-                    greet(li + d, lon_at(j))
-            guarded(d, hello)
-        for j in range(1, n_lon):
-            greet(li, lon_at(j))
+        @pl.when(sides == 1)
+        def _():
+            greet(jnp.where(li == 0, n_lat - 1, 0), lo)
+        greeted = greeted + n_lat - 3 + (sides == 1).astype(jnp.int32)
 
     for copy in small:
         copy.wait()
@@ -151,11 +153,18 @@
     for d in (-1, 0, 1):
         code_out[d + 1] = (code_line - clat * d).astype(F32)
 
-    if direct:
-        pl.semaphore_wait(barrier, n_all - 1)
-    else:
-        sides = (li > 0).astype(jnp.int32) + (li < n_lat - 1).astype(jnp.int32)
-        pl.semaphore_wait(barrier, (n_lon - 1) + (n_lat - 1) + sides * (n_lon - 1))
+    pl.semaphore_wait(barrier, greeted)
+
+    rounds = n_lat - 2 if direct else 0
+
+    def news(k):
+        if 0 < k <= rounds:
+            for d in (-1, 1):
+                guarded(-d, lambda d=d: pl.semaphore_wait(token.at[(1 - d) // 2], 1))
+        if k < rounds:
+            for d in (-1, 1):
+                guarded(d, lambda d=d: pl.semaphore_signal(
+                    token.at[(1 - d) // 2], inc=1, device_id={"lat": li + d, "lon": lo}, device_id_type=MESH))
 
     def wide(kind, d, j, src, dst):
         return pltpu.make_async_remote_copy(
@@ -230,6 +239,7 @@
 
     start_wide(ask_make)
     start_wide(code_make)
+    news(0)
     codes[n_lon + lo] = code_out[1]
 
     flow_copy.wait()
@@ -348,6 +358,7 @@
         for j in js:
             respond(d, j)
 
+    news(1)
     pad = terms.shape[1] - n_src
     if pad:
         for rnd in range(3):
@@ -442,6 +453,7 @@
 
     recv_wide(4, cap)
     load_window(0)
+    news(2)
 
     def unpack(sources, offset, first):
         for o in range(n_lon):
@@ -458,6 +470,7 @@
     own_strips = [strip_in[o] for o in range(n_lon)]
     for k in range(clat // HALO):
         unpack(own_strips, k * middle, (k + 1) * HALO)
+    news(3)
     recv_rows(3, 0, n_lon * HALO // 2)
     for k in range(2):
         edges = []
@@ -590,7 +603,9 @@
 
     p1 = window_model()
     spread(1, [weight_wide[b] * p1[b] for b in range(cap)])
+    news(4)
     build_dense()
+    news(5)
     recv_wide(5, cap)
     load_window(1)
     g1 = window_model()
@@ -600,6 +615,8 @@
     line = jnp.zeros((1, clon), F32)
     for n, value in enumerate((pltpu.roll(columns, clon - cap, 1) * p_all, u_all * p_all, u_all * g_all, columns * g_all * g_all)):
         line = line + pltpu.roll(jnp.sum(value, axis=0, keepdims=True), n * cap, 1)
+    for k in range(6, max(rounds, 6) + 1):
+        news(k)
     reduce_start(line)
     recv_dense()
     dense(0)
@@ -718,6 +735,7 @@
             dma, dma, dma,
             dma((3,)), dma((8,)), dma, dma((3, n_lon)),
             dma((4,)),
+            pltpu.SemaphoreType.REGULAR((2,)),
             f32(1, cap, clon), f32(1, cap, clon),
             i32(1, cap), i32(1, cap), i32(1, 1),
             dma((5,)),

time: 27.9 us -> 27.3 us (0.978)
  Pallas kernels: 26.5 us -> 25.9 us
    pallas_call x1, Pallas kernels: 25.8 us -> 25.2 us  [shards(): pl.pallas_call(functools.partial(kernel, n_lat, n_lon), out_shape=(f32(*f...]
where the time goes in v5:
time: 27.3 us; the launch traced here: 27.2 us
  Pallas kernels  25.9 us (95%)
  between operations  1.29 us (5%)
    pallas_call x1, Pallas kernels, shards(): pl.pallas_call(functools.partial(kernel, n_lat, n_lon), out_shape=(f32(*f...  25.2 us
    pallas_call x1, Pallas kernels, shards(): pl.pallas_call(store_kernel, out_shape=(out, out), in_specs=[anywhere] *...  0.72 us

profile of v5, /device:TPU:0, one launch (start us, length us, event | category | flops | bytes accessed | tf_op | source)
XLA Modules:
  0.0 27.2 jit_solution(5471350427604382894)
XLA Ops:
  1.3 25.2 %shard_map.86 = (f32[256,128]{1,0:T(8,128)S(1)}, f32[256,128]{1,0:T(8,128)S(1)}) custom-call(f32[2,16,16,128]{3,2,1,0:T(8,128)} %courant.1, f32[512,128]{1,0:T(8,128)} %bitcast.4, f32[1,8,128,128]{3,2,1,0:T(8,128)} %obs.1, f32[1,8,128]{2,1,0:T(8,128)} %weight_in.1, f32[1,8,128]{2,1,0:T(8,128)} %innov_in.1, s32[1,8]{1,0:T(1,128)} %bitcast.5, s32[1,8]{1,0:T(1,128)} %row_in.1, ...), custom_call_target="tpu_custom_call" | custom-call | tf_op jit(solution)/shard_map/pallas_call | solution.py:694
  26.4 0.7 %shard_map.87 = (f32[256,128]{1,0:T(8,128)}, f32[256,128]{1,0:T(8,128)}) custom-call(f32[256,128]{1,0:T(8,128)S(1)} %get-tuple-element.6.inc, f32[256,128]{1,0:T(8,128)S(1)} %get-tuple-element.7.res), custom_call_target="tpu_custom_call" | custom-call | tf_op jit(solution)/shard_map/pallas_call | solution.py:746

commit v6 on v5

--- a/solution.py
+++ b/solution.py
@@ -354,7 +354,7 @@
     answer(0, 0)
     near = [j for j in range(1, n_lon) if 2 * j != n_lon]
     far = [j for j in range(1, n_lon) if 2 * j == n_lon]
-    for d, js in ((1, [0]), (-1, [0]), (1, near), (-1, near), (0, near), (1, far), (-1, far), (0, far)):
+    for d, js in ((0, near), (1, [0]), (-1, [0]), (1, near), (-1, near), (1, far), (-1, far), (0, far)):
         for j in js:
             respond(d, j)
 
@@ -576,7 +576,7 @@
         if direct:
             me = li * n_lon + lo
             red_far[me] = line
-            for j in range(1, n_all):
+            for j in sorted(range(1, n_all), key=lambda j: abs(2 * j - n_all)):
                 other = lax.rem(me + j, n_all)
                 red_make(2, red_far, me, lax.div(other, n_lon), lax.rem(other, n_lon)).start()
         else:
@@ -601,23 +601,26 @@
             tile = jnp.where(lane == b, cols[b], tile)
         return tile
 
+    def line_of(value, n):
+        return pltpu.roll(jnp.sum(value, axis=0, keepdims=True), n * cap, 1)
+
     p1 = window_model()
     spread(1, [weight_wide[b] * p1[b] for b in range(cap)])
     news(4)
     build_dense()
+    p_all = packed(p1)
+    u_all = columns * p_all
     news(5)
+    line = line_of(pltpu.roll(columns, clon - cap, 1) * p_all, 0) + line_of(u_all * p_all, 1)
     recv_wide(5, cap)
     load_window(1)
     g1 = window_model()
-    spread(2, [weight_wide[b] * g1[b] for b in range(cap)])
-    p_all, g_all = packed(p1), packed(g1)
-    u_all = columns * p_all
-    line = jnp.zeros((1, clon), F32)
-    for n, value in enumerate((pltpu.roll(columns, clon - cap, 1) * p_all, u_all * p_all, u_all * g_all, columns * g_all * g_all)):
-        line = line + pltpu.roll(jnp.sum(value, axis=0, keepdims=True), n * cap, 1)
+    g_all = packed(g1)
+    line = line + line_of(u_all * g_all, 2) + line_of(columns * g_all * g_all, 3)
     for k in range(6, max(rounds, 6) + 1):
         news(k)
     reduce_start(line)
+    spread(2, [weight_wide[b] * g1[b] for b in range(cap)])
     recv_dense()
     dense(0)
     reduce_turn()

time: 27.3 us -> 26.9 us (0.985)
  Pallas kernels: 25.9 us -> 25.5 us
    pallas_call x1, Pallas kernels: 25.2 us -> 24.7 us  [shards(): pl.pallas_call(functools.partial(kernel, n_lat, n_lon), out_shape=(f32(*f...]
where the time goes in v6:
time: 26.9 us; the launch traced here: 26.8 us
  Pallas kernels  25.5 us (95%)
  between operations  1.29 us (5%)
    pallas_call x1, Pallas kernels, shards(): pl.pallas_call(functools.partial(kernel, n_lat, n_lon), out_shape=(f32(*f...  24.7 us
    pallas_call x1, Pallas kernels, shards(): pl.pallas_call(store_kernel, out_shape=(out, out), in_specs=[anywhere] *...  0.72 us

profile of v6, /device:TPU:0, one launch (start us, length us, event | category | flops | bytes accessed | tf_op | source)
XLA Modules:
  0.0 26.8 jit_solution(1778739225746948369)
XLA Ops:
  1.3 24.7 %shard_map.86 = (f32[256,128]{1,0:T(8,128)S(1)}, f32[256,128]{1,0:T(8,128)S(1)}) custom-call(f32[2,16,16,128]{3,2,1,0:T(8,128)} %courant.1, f32[512,128]{1,0:T(8,128)} %bitcast.4, f32[1,8,128,128]{3,2,1,0:T(8,128)} %obs.1, f32[1,8,128]{2,1,0:T(8,128)} %weight_in.1, f32[1,8,128]{2,1,0:T(8,128)} %innov_in.1, s32[1,8]{1,0:T(1,128)} %bitcast.5, s32[1,8]{1,0:T(1,128)} %row_in.1, ...), custom_call_target="tpu_custom_call" | custom-call | tf_op jit(solution)/shard_map/pallas_call | solution.py:697
  26.0 0.7 %shard_map.87 = (f32[256,128]{1,0:T(8,128)}, f32[256,128]{1,0:T(8,128)}) custom-call(f32[256,128]{1,0:T(8,128)S(1)} %get-tuple-element.6.inc, f32[256,128]{1,0:T(8,128)S(1)} %get-tuple-element.7.res), custom_call_target="tpu_custom_call" | custom-call | tf_op jit(solution)/shard_map/pallas_call | solution.py:749
